TPU v7x, 32 devices: a whole 2x2x4 slice. The times are simulated.
32 devices in a mesh: pts: 8 (over y, x, core), cam: 4 (over z).
Axes of the slice: x: 2, y: 2, z: 4, core: 2. Of those that a mesh axis runs over, the one named last changes fastest.
Arguments:
- cameras: float32 [9, 4096], P(None, ('pts', 'cam')), may hold values from -0.5 to 2
- increment: float32 [9, 4096], P(None, ('pts', 'cam')), may hold values from -0.3 to 0.3
- points: float32 [3, 524288], P(None, 'pts'), may hold values from -6 to 2
- point_gradient: float32 [3, 524288], P(None, 'pts'), may hold values from -1.8 to 1.8
- point_inverse: float32 [9, 524288], P(None, 'pts'), may hold values from -0.35 to 1.6, as said below
- cam_jacobian: bfloat16 [18, 8388608], P(None, ('pts', 'cam')), may hold values from -3 to 3
- point_jacobian: bfloat16 [6, 8388608], P(None, ('pts', 'cam')), may hold values from -3 to 3
- observed: float32 [2, 8388608], P(None, ('pts', 'cam')), may hold values from -10 to 10
- tile_block: int32 [32768], P(('pts', 'cam')), may hold values from 0 to 31
- tile_points: int32 [32768], P(('pts', 'cam')), may hold values from 0 to 255
- obs_camera: int32 [8388608], P(('pts', 'cam')), may hold values from 0 to 127
- obs_point: int32 [8388608], P(('pts', 'cam')), may hold values from 0 to 255
- accept: int32 [], replicated, may hold values from 0 to 1073741823
Outputs:
- residual: float32 [2, 8388608], P(None, ('pts', 'cam'))
- trial_cost: float32 [], replicated
- accepted_points: float32 [3, 524288], P(None, 'pts')
- accepted_cameras: float32 [9, 4096], P(None, ('pts', 'cam'))
Inputs may be any that keep to these rules, and one draw needn't show every extreme that they name: `tile_block`: the block of 128 cameras that all 256 observations of a tile look at. `tile_points`: the block of 256 points of its point group that all 256 observations of a tile look at. `obs_camera`: an observation's camera within its tile's block. `obs_point`: an observation's point within its tile's point block. `accept`: an odd word accepts the step, an even one keeps the old parameters. `point_inverse`: each 3 x 3 block is symmetric with a dominant positive diagonal.
All inputs are finite; a program needn't handle non-finite values.
Results may differ from a plain program's by a relative error of at most 0.0003.
Values sent between devices are 32-bit elements; how exact they have to be, the bound alone decides.
No kernel may reach another device: no remote copies, remote signals or barrier semaphores. Data moves between devices by JAX's collectives and lax.ppermute only.
A program may use at most 192 MiB of HBM per device.

v0:
```python
import math

import jax
import jax.numpy as jnp
from jax import lax
from jax.sharding import PartitionSpec as P

CB = 128
PB = 256
TILE = 256


def rotate_point(angles, coords):
    angle_size = jnp.sqrt(jnp.sum(angles * angles, axis=0))
    cosine = jnp.cos(angle_size)
    sine_ratio = jnp.sinc(angle_size / math.pi)
    cosine_ratio = 0.5 * jnp.square(jnp.sinc(angle_size / (2.0 * math.pi)))
    crossed = jnp.stack(
        [
            angles[1] * coords[2] - angles[2] * coords[1],
            angles[2] * coords[0] - angles[0] * coords[2],
            angles[0] * coords[1] - angles[1] * coords[0],
        ]
    )
    inner_part = jnp.sum(angles * coords, axis=0)
    return cosine * coords + sine_ratio * crossed + cosine_ratio * inner_part * angles


def project(camera, coords):
    placed = rotate_point(camera[0:3], coords) + camera[3:6]
    depth_clip = jnp.maximum(-placed[2], 1.0)
    planar = placed[0:2] / depth_clip
    radius = jnp.sum(planar * planar, axis=0)
    factor = camera[6] * (1.0 + camera[7] * radius + camera[8] * radius * radius)
    return factor * planar


def couple(cam_rows, point_rows, cam_steps):
    cam_rows = cam_rows.astype(jnp.float32)
    point_rows = point_rows.astype(jnp.float32)
    first_row = jnp.sum(cam_rows[0:9] * cam_steps, axis=0)
    second_row = jnp.sum(cam_rows[9:18] * cam_steps, axis=0)
    return point_rows[0:3] * first_row + point_rows[3:6] * second_row


def solve_points(inverse, gradient, reduced):
    residue = gradient - reduced
    return jnp.stack(
        [
            inverse[3 * target] * residue[0]
            + inverse[3 * target + 1] * residue[1]
            + inverse[3 * target + 2] * residue[2]
            for target in range(3)
        ]
    )


def tile_onehot(local_ids, per_turn, width):
    columns = lax.iota(jnp.int32, width)
    return (local_ids.reshape(per_turn, 1, TILE) == columns.reshape(1, width, 1)).astype(
        jnp.float32
    )


def block_select(block_ids, first, count):
    columns = lax.iota(jnp.int32, count) + first
    return (block_ids.reshape(-1, 1) == columns.reshape(1, count)).astype(jnp.float32)


def reduce_range(coupling, tile_points, obs_point, first, count, per_turn, turn_count):

    def add_turn(turn, total):
        chosen = lax.dynamic_slice_in_dim(tile_points, turn * per_turn, per_turn, 0)
        local_ids = lax.dynamic_slice_in_dim(obs_point, turn * per_turn * TILE, per_turn * TILE, 0)
        values = lax.dynamic_slice_in_dim(coupling, turn * per_turn * TILE, per_turn * TILE, 1)
        inside = jnp.einsum(
            "rgt,gpt->rgp",
            values.reshape(3, per_turn, TILE),
            tile_onehot(local_ids, per_turn, PB),
            precision=lax.Precision.HIGHEST,
        )
        return total + jnp.einsum(
            "rgp,gb->rbp",
            inside,
            block_select(chosen, first, count),
            precision=lax.Precision.HIGHEST,
        )

    summed = lax.fori_loop(0, turn_count, add_turn, jnp.zeros((3, count, PB), jnp.float32))
    return summed.reshape(3, count * PB)


def on_device(
    cameras,
    increment,
    points,
    point_gradient,
    point_inverse,
    cam_jacobian,
    point_jacobian,
    observed,
    tile_block,
    tile_points,
    obs_camera,
    obs_point,
    accept,
):
    trial_cameras = cameras + increment
    group_trial, group_steps = (
        lax.all_gather(trial_cameras, "cam", axis=1, tiled=True),
        lax.all_gather(increment, "cam", axis=1, tiled=True),
    )
    every_trial, every_steps = (
        lax.all_gather(group_trial, "pts", axis=1, tiled=True),
        lax.all_gather(group_steps, "pts", axis=1, tiled=True),
    )
    stacked = jnp.concatenate([every_trial, every_steps], axis=0)
    cam_blocks = stacked.shape[1] // CB
    blocks = stacked.reshape(18, cam_blocks, CB)
    tile_count = tile_block.shape[0]
    obs_count = obs_camera.shape[0]
    per_turn = math.gcd(tile_count, 64)
    turn_count = tile_count // per_turn

    def lookup(turn, gathered):
        chosen = lax.dynamic_slice_in_dim(tile_block, turn * per_turn, per_turn, 0)
        cam_local = lax.dynamic_slice_in_dim(obs_camera, turn * per_turn * TILE, per_turn * TILE, 0)
        slabs = jnp.einsum(
            "rbc,gb->rgc",
            blocks,
            block_select(chosen, 0, cam_blocks),
            precision=lax.Precision.HIGHEST,
        )
        values = jnp.einsum(
            "rgc,gct->rgt",
            slabs,
            tile_onehot(cam_local, per_turn, CB),
            precision=lax.Precision.HIGHEST,
        )
        return lax.dynamic_update_slice_in_dim(
            gathered, values.reshape(18, per_turn * TILE), turn * per_turn * TILE, 1
        )

    per_obs = lax.fori_loop(0, turn_count, lookup, jnp.zeros((18, obs_count), jnp.float32))
    coupling = couple(cam_jacobian, point_jacobian, per_obs[9:18])
    point_count = points.shape[1]
    point_blocks = point_count // PB
    reduced = reduce_range(coupling, tile_points, obs_point, 0, point_blocks, per_turn, turn_count)
    summed = lax.psum(reduced, "cam")
    point_step = solve_points(point_inverse, point_gradient, summed)
    trial_blocks = (points + point_step).reshape(3, point_blocks, PB)

    def fetch(turn, gathered):
        chosen = lax.dynamic_slice_in_dim(tile_points, turn * per_turn, per_turn, 0)
        local_ids = lax.dynamic_slice_in_dim(obs_point, turn * per_turn * TILE, per_turn * TILE, 0)
        slabs = jnp.einsum(
            "rbp,gb->rgp",
            trial_blocks,
            block_select(chosen, 0, point_blocks),
            precision=lax.Precision.HIGHEST,
        )
        values = jnp.einsum(
            "rgp,gpt->rgt",
            slabs,
            tile_onehot(local_ids, per_turn, PB),
            precision=lax.Precision.HIGHEST,
        )
        return lax.dynamic_update_slice_in_dim(
            gathered, values.reshape(3, per_turn * TILE), turn * per_turn * TILE, 1
        )

    seen_points = lax.fori_loop(0, turn_count, fetch, jnp.zeros((3, obs_count), jnp.float32))
    residual = project(per_obs[0:9], seen_points) - observed
    cost_sum = lax.psum(jnp.sum(residual * residual), ("pts", "cam"))
    obs_total = observed.shape[1] * lax.axis_size(("pts", "cam"))
    trial_cost = cost_sum / (2.0 * obs_total)
    accepted_flag = jnp.remainder(accept, 2).astype(jnp.float32)
    return (
        residual,
        trial_cost,
        points + accepted_flag * point_step,
        cameras + accepted_flag * increment,
    )


def solution(mesh):
    in_specs = (
        P(None, ("pts", "cam")),
        P(None, ("pts", "cam")),
        P(None, "pts"),
        P(None, "pts"),
        P(None, "pts"),
        P(None, ("pts", "cam")),
        P(None, ("pts", "cam")),
        P(None, ("pts", "cam")),
        P(("pts", "cam")),
        P(("pts", "cam")),
        P(("pts", "cam")),
        P(("pts", "cam")),
        P(),
    )
    out_specs = (P(None, ("pts", "cam")), P(), P(None, "pts"), P(None, ("pts", "cam")))
    return jax.shard_map(
        on_device, mesh=mesh, in_specs=in_specs, out_specs=out_specs, check_vma=False
    )
```

profile of v0, /device:TPU:0, one launch (start us, length us, event | category | flops | bytes accessed | tf_op | source)
XLA Modules:
  0.0 726.2 jit_solution(1532738634116308873)
XLA Ops:
  7.9 15.1 %all_gather.14 = f32[9,512]{1,0:T(8,128)S(1)} all-gather(f32[9,128]{1,0:T(8,128)} %param.21), channel_id=1, replica_groups=mesh['pts'=8,'cam'=4] {'cam'}, dimensions={1}, use_global_device_ids=true | all-gather | bytes 23040 | tf_op jit(solution)/shard_map/all_gather | solution.py:111
  24.3 13.2 %all_gather.12 = f32[9,512]{1,0:T(8,128)S(1)} all-gather(f32[9,128]{1,0:T(8,128)S(1)} %get-tuple-element.472), channel_id=1, replica_groups=mesh['pts'=8,'cam'=4] {'cam'}, dimensions={1}, use_global_device_ids=true | all-gather | bytes 23040 | tf_op jit(solution)/shard_map/all_gather | solution.py:110
  37.4 9.3 %all_gather.13 = f32[9,4096]{1,0:T(8,128)S(1)} all-gather(f32[9,512]{1,0:T(8,128)S(1)} %all_gather.12), channel_id=1, replica_groups=mesh['pts'=8,'cam'=4] {'pts'}, dimensions={1}, use_global_device_ids=true | all-gather | bytes 165888 | tf_op jit(solution)/shard_map/all_gather | solution.py:114
  46.7 9.3 %all_gather.15 = f32[9,4096]{1,0:T(8,128)S(1)} all-gather(f32[9,512]{1,0:T(8,128)S(1)} %all_gather.14), channel_id=1, replica_groups=mesh['pts'=8,'cam'=4] {'pts'}, dimensions={1}, use_global_device_ids=true | all-gather | bytes 165888 | tf_op jit(solution)/shard_map/all_gather | solution.py:115
  56.1 8.5 %broadcast_in_dim.9 = f32[18,262144]{1,0:T(8,128)} broadcast(f32[]{:T(128)} %constant.230.clone.1), dimensions={} | broadcast | bytes 18874372 | tf_op jit(solution)/shard_map/broadcast_in_dim | solution.py:144
  64.6 125.2 %while.46 = (s32[]{:T(128)}, f32[18,262144]{1,0:T(8,128)}, s32[262144]{0:T(1024)}, s32[1024]{0:T(1024)}, f32[18,32,128]{2,1,0:T(8,128)S(1)}, /*index=5*/s32[]{:T...) while((s32[]{:T(128)}, f32[18,262144]{1,0:T(8,128)}, ...), condition=%wide.region_1.0_spmd, body=%wide.region_0.0_spmd.sunk | while | flops 511707136 | bytes 13992929 | solution.py:144
  189.8 14.4 %convert_element_type.31 = f32[18,262144]{1,0:T(8,128)} convert(bf16[18,262144]{1,0:T(8,128)(2,1)} %param.25) | non-fusion elementwise | flops 4718592 | bytes 28311552 | tf_op jit(solution)/shard_map/convert_element_type | solution.py:39
  204.9 19.1 %fusion.26 = (f32[262144]{0:T(1024)S(1)}, f32[262144]{0:T(1024)S(1)}) fusion(f32[18,262144]{1,0:T(8,128)} %convert_element_type.31, f32[18,262144]{1,0:T(8,128)} %get-tuple-element.401), kind=kLoop, calls=%fused_computation.35 | loop fusion | flops 8912896 | bytes 30408704 | tf_op jit(solution)/shard_map/reduce_sum | solution.py:41
  227.2 174.9 %while.48 = (s32[]{:T(128)}, f32[3,256,256]{2,1,0:T(8,128)S(1)}, s32[1024]{0:T(1024)}, s32[262144]{0:T(1024)}, f32[3,262144]{1,0:T(4,128)}, /*index=5*/s32[]{:T(...) while((s32[]{:T(128)}, f32[3,256,256]{2,1,0:T(8,128)S(1)}, ...), condition=%wide.region_6.0_spmd.clone, body=%wide.region_5.0_spmd.clone.sunk | while | flops 306593792 | bytes 2884575 | solution.py:89
  229.3 7.5 %fusion.93 = f32[64,256,3]{1,2,0:T(4,128)S(1)} fusion(f32[3,64,256]{2,0,1:T(4,128)S(1)} %bitcast.80, s32[64,256]{1,0:T(8,128)S(1)} %eq.437), kind=kOutput, calls=%fused_computation.22.clone.1 | convolution fusion | flops 155189248 | bytes 458752 | tf_op jit(solution)/shard_map/while/body/eval_jaxpr/rgt,gpt->rgp/dot_general | solution.py:76
  240.3 7.5 %fusion.93 = f32[64,256,3]{1,2,0:T(4,128)S(1)} fusion(f32[3,64,256]{2,0,1:T(4,128)S(1)} %bitcast.80, s32[64,256]{1,0:T(8,128)S(1)} %eq.437), kind=kOutput, calls=%fused_computation.22.clone.1 | convolution fusion | flops 155189248 | bytes 458752 | tf_op jit(solution)/shard_map/while/body/eval_jaxpr/rgt,gpt->rgp/dot_general | solution.py:76
  251.2 7.5 %fusion.93 = f32[64,256,3]{1,2,0:T(4,128)S(1)} fusion(f32[3,64,256]{2,0,1:T(4,128)S(1)} %bitcast.80, s32[64,256]{1,0:T(8,128)S(1)} %eq.437), kind=kOutput, calls=%fused_computation.22.clone.1 | convolution fusion | flops 155189248 | bytes 458752 | tf_op jit(solution)/shard_map/while/body/eval_jaxpr/rgt,gpt->rgp/dot_general | solution.py:76
  262.1 7.5 %fusion.93 = f32[64,256,3]{1,2,0:T(4,128)S(1)} fusion(f32[3,64,256]{2,0,1:T(4,128)S(1)} %bitcast.80, s32[64,256]{1,0:T(8,128)S(1)} %eq.437), kind=kOutput, calls=%fused_computation.22.clone.1 | convolution fusion | flops 155189248 | bytes 458752 | tf_op jit(solution)/shard_map/while/body/eval_jaxpr/rgt,gpt->rgp/dot_general | solution.py:76
  273.0 7.5 %fusion.93 = f32[64,256,3]{1,2,0:T(4,128)S(1)} fusion(f32[3,64,256]{2,0,1:T(4,128)S(1)} %bitcast.80, s32[64,256]{1,0:T(8,128)S(1)} %eq.437), kind=kOutput, calls=%fused_computation.22.clone.1 | convolution fusion | flops 155189248 | bytes 458752 | tf_op jit(solution)/shard_map/while/body/eval_jaxpr/rgt,gpt->rgp/dot_general | solution.py:76
  283.9 7.5 %fusion.93 = f32[64,256,3]{1,2,0:T(4,128)S(1)} fusion(f32[3,64,256]{2,0,1:T(4,128)S(1)} %bitcast.80, s32[64,256]{1,0:T(8,128)S(1)} %eq.437), kind=kOutput, calls=%fused_computation.22.clone.1 | convolution fusion | flops 155189248 | bytes 458752 | tf_op jit(solution)/shard_map/while/body/eval_jaxpr/rgt,gpt->rgp/dot_general | solution.py:76
  294.8 7.5 %fusion.93 = f32[64,256,3]{1,2,0:T(4,128)S(1)} fusion(f32[3,64,256]{2,0,1:T(4,128)S(1)} %bitcast.80, s32[64,256]{1,0:T(8,128)S(1)} %eq.437), kind=kOutput, calls=%fused_computation.22.clone.1 | convolution fusion | flops 155189248 | bytes 458752 | tf_op jit(solution)/shard_map/while/body/eval_jaxpr/rgt,gpt->rgp/dot_general | solution.py:76
  305.8 7.5 %fusion.93 = f32[64,256,3]{1,2,0:T(4,128)S(1)} fusion(f32[3,64,256]{2,0,1:T(4,128)S(1)} %bitcast.80, s32[64,256]{1,0:T(8,128)S(1)} %eq.437), kind=kOutput, calls=%fused_computation.22.clone.1 | convolution fusion | flops 155189248 | bytes 458752 | tf_op jit(solution)/shard_map/while/body/eval_jaxpr/rgt,gpt->rgp/dot_general | solution.py:76
  316.7 7.5 %fusion.93 = f32[64,256,3]{1,2,0:T(4,128)S(1)} fusion(f32[3,64,256]{2,0,1:T(4,128)S(1)} %bitcast.80, s32[64,256]{1,0:T(8,128)S(1)} %eq.437), kind=kOutput, calls=%fused_computation.22.clone.1 | convolution fusion | flops 155189248 | bytes 458752 | tf_op jit(solution)/shard_map/while/body/eval_jaxpr/rgt,gpt->rgp/dot_general | solution.py:76
  327.6 7.5 %fusion.93 = f32[64,256,3]{1,2,0:T(4,128)S(1)} fusion(f32[3,64,256]{2,0,1:T(4,128)S(1)} %bitcast.80, s32[64,256]{1,0:T(8,128)S(1)} %eq.437), kind=kOutput, calls=%fused_computation.22.clone.1 | convolution fusion | flops 155189248 | bytes 458752 | tf_op jit(solution)/shard_map/while/body/eval_jaxpr/rgt,gpt->rgp/dot_general | solution.py:76
  338.5 7.5 %fusion.93 = f32[64,256,3]{1,2,0:T(4,128)S(1)} fusion(f32[3,64,256]{2,0,1:T(4,128)S(1)} %bitcast.80, s32[64,256]{1,0:T(8,128)S(1)} %eq.437), kind=kOutput, calls=%fused_computation.22.clone.1 | convolution fusion | flops 155189248 | bytes 458752 | tf_op jit(solution)/shard_map/while/body/eval_jaxpr/rgt,gpt->rgp/dot_general | solution.py:76
  349.4 7.5 %fusion.93 = f32[64,256,3]{1,2,0:T(4,128)S(1)} fusion(f32[3,64,256]{2,0,1:T(4,128)S(1)} %bitcast.80, s32[64,256]{1,0:T(8,128)S(1)} %eq.437), kind=kOutput, calls=%fused_computation.22.clone.1 | convolution fusion | flops 155189248 | bytes 458752 | tf_op jit(solution)/shard_map/while/body/eval_jaxpr/rgt,gpt->rgp/dot_general | solution.py:76
  360.3 7.5 %fusion.93 = f32[64,256,3]{1,2,0:T(4,128)S(1)} fusion(f32[3,64,256]{2,0,1:T(4,128)S(1)} %bitcast.80, s32[64,256]{1,0:T(8,128)S(1)} %eq.437), kind=kOutput, calls=%fused_computation.22.clone.1 | convolution fusion | flops 155189248 | bytes 458752 | tf_op jit(solution)/shard_map/while/body/eval_jaxpr/rgt,gpt->rgp/dot_general | solution.py:76
  371.3 7.5 %fusion.93 = f32[64,256,3]{1,2,0:T(4,128)S(1)} fusion(f32[3,64,256]{2,0,1:T(4,128)S(1)} %bitcast.80, s32[64,256]{1,0:T(8,128)S(1)} %eq.437), kind=kOutput, calls=%fused_computation.22.clone.1 | convolution fusion | flops 155189248 | bytes 458752 | tf_op jit(solution)/shard_map/while/body/eval_jaxpr/rgt,gpt->rgp/dot_general | solution.py:76
  382.2 7.5 %fusion.93 = f32[64,256,3]{1,2,0:T(4,128)S(1)} fusion(f32[3,64,256]{2,0,1:T(4,128)S(1)} %bitcast.80, s32[64,256]{1,0:T(8,128)S(1)} %eq.437), kind=kOutput, calls=%fused_computation.22.clone.1 | convolution fusion | flops 155189248 | bytes 458752 | tf_op jit(solution)/shard_map/while/body/eval_jaxpr/rgt,gpt->rgp/dot_general | solution.py:76
  393.1 7.5 %fusion.93 = f32[64,256,3]{1,2,0:T(4,128)S(1)} fusion(f32[3,64,256]{2,0,1:T(4,128)S(1)} %bitcast.80, s32[64,256]{1,0:T(8,128)S(1)} %eq.437), kind=kOutput, calls=%fused_computation.22.clone.1 | convolution fusion | flops 155189248 | bytes 458752 | tf_op jit(solution)/shard_map/while/body/eval_jaxpr/rgt,gpt->rgp/dot_general | solution.py:76
  403.7 52.0 %all-reduce.2.cloned.1.call-done = f32[3,65536]{1,0:T(4,128)} async-done(((f32[3,65536]{1,0:T(4,128)}), f32[3,65536]{1,0:T(4,128)}) %all-reduce.2.cloned.1.call-update) | async-done | bytes 786448 | tf_op jit(solution)/shard_map/psum | solution.py:149
  457.2 10.3 %multiply_add_fusion.5 = (f32[1,65536]{1,0:T(1,128)S(1)}, f32[1,65536]{1,0:T(1,128)S(1)}, f32[1,65536]{1,0:T(1,128)S(1)}) fusion(f32[9,65536]{1,0:T(8,128)} %param.24, f32[3,65536]{1,0:T(4,128)S(1)} %sub.24), kind=kLoop, calls=%fused_computation.114 | loop fusion | flops 983040 | bytes 3932160 | tf_op jit(solution)/shard_map/add | solution.py:50
  471.8 131.6 %while.47 = (s32[]{:T(128)}, f32[3,262144]{1,0:T(4,128)}, s32[262144]{0:T(1024)}, s32[1024]{0:T(1024)}, f32[3,256,256]{2,1,0:T(8,128)S(1)}, /*index=5*/s32[]{:T(...) while((s32[]{:T(128)}, f32[3,262144]{1,0:T(4,128)}, s32[262144]{0:T(1024)}, ...), condition=%wide.region_9.0_spmd, body=%wide.region_8.0_spmd.sunk | while | flops 306200576 | bytes 2163669 | solution.py:172
  474.1 5.4 fusion.89
  482.3 5.4 fusion.89
  490.5 5.4 fusion.89
  498.8 5.4 fusion.89
  507.0 5.4 fusion.89
  515.2 5.4 fusion.89
  523.4 5.4 fusion.89
  531.6 5.4 fusion.89
  539.8 5.4 fusion.89
  548.1 5.4 fusion.89
  556.3 5.4 fusion.89
  564.5 5.4 fusion.89
  580.9 5.4 fusion.89
  603.4 13.8 %multiply_reduce_fusion.1 = (f32[262144]{0:T(1024)S(1)}, f32[262144]{0:T(1024)S(1)}) fusion(f32[18,262144]{1,0:T(8,128)} %get-tuple-element.401, f32[3,262144]{1,0:T(4,128)} %get-tuple-element.403), kind=kLoop, calls=%fused_computation.44 | loop fusion | flops 2621440 | bytes 8388608 | tf_op jit(solution)/shard_map/reduce_sum | solution.py:14
  617.2 16.9 %multiply_subtract_fusion.3 = (f32[1,262144]{1,0:T(1,128)S(1)}, f32[1,262144]{1,0:T(1,128)S(1)}, f32[1,262144]{1,0:T(1,128)S(1)}) fusion(f32[3,262144]{1,0:T(4,128)} %get-tuple-element.403, f32[18,262144]{1,0:T(8,128)} %get-tuple-element.401), kind=kLoop, calls=%fused_computation.107 | loop fusion | flops 2359296 | bytes 9437184 | tf_op jit(solution)/shard_map/sub | solution.py:20
  634.1 6.1 sqrt_cosine_fusion
  640.2 12.1 %fusion.30 = f32[3,262144]{1,0:T(4,128)S(1)} fusion(f32[1,262144]{1,0:T(1,128)S(1)} %get-tuple-element.462, f32[1,262144]{1,0:T(1,128)S(1)} %get-tuple-element.461, f32[1,262144]{1,0:T(1,128)S(1)} %get-tuple-element.460, f32[18,262144]{1,0:T(8,128)} %get-tuple-element.401, f32[3,262144]{1,0:T(4,128)} %get-tuple-element.403, ...), kind=kLoop, calls=%fused_computation.42 | loop fusion | flops 6291456 | bytes 18874368 | tf_op jit(solution)/shard_map/add | solution.py:30
  653.8 9.1 %multiply_reduce_fusion.3 = (f32[262144]{0:T(1024)S(1)}, f32[2,262144]{1,0:T(2,128)S(1)}) fusion(f32[262144]{0:T(1024)S(1)} %bitcast.85, f32[3,262144]{1,0:T(4,128)S(1)} %fusion.30), kind=kLoop, calls=%fused_computation.48 | loop fusion | flops 1310720 | bytes 6291456 | tf_op jit(solution)/shard_map/reduce_sum | solution.py:33
  663.0 10.0 %fusion.47 = f32[1,262144]{1,0:T(1,128)S(1)} fusion(f32[1,262144]{1,0:T(1,128)S(1)} %bitcast.83, f32[18,262144]{1,0:T(8,128)} %get-tuple-element.401), kind=kLoop, calls=%fused_computation.78 | loop fusion | flops 1572864 | bytes 5242880 | tf_op jit(solution)/shard_map/mul | solution.py:34
  677.0 40.1 %psum.15 = f32[]{:T(128)} all-reduce(f32[]{:T(128)} %get-tuple-element.456), channel_id=1, replica_groups=mesh['pts'=8,'cam'=4] {'pts','cam'}, use_global_device_ids=true, to_apply=%region_13.15 | all-reduce | flops 1 | bytes 8 | tf_op jit(solution)/shard_map/psum | solution.py:174
  (331 shorter events, 258.5 us)
Async XLA Ops:
  7.2 448.5 %all-reduce.2.cloned.1.call-start = ((), (), s32[]{:S(2)}) async-start(), calls=%async_computation | async-start | bytes 2097152 | tf_op jit(solution)/shard_map/psum | solution.py:149
  189.8 14.5 %copy-start = (bf16[6,262144]{1,0:T(8,128)(2,1)S(1)}, bf16[6,262144]{1,0:T(8,128)(2,1)}, u32[]{:S(2)}) copy-start(bf16[6,262144]{1,0:T(8,128)(2,1)} %param.26) | copy-start | bytes 9437188
  227.2 228.5 %copy-start.2 = (f32[3,65536]{1,0:T(4,128)S(1)}, f32[3,65536]{1,0:T(4,128)}, u32[]{:S(2)}) copy-start(f32[3,65536]{1,0:T(4,128)} %param.23) | copy-start | bytes 2359300
  403.6 63.9 %copy-start.3 = (f32[3,65536]{1,0:T(4,128)S(1)}, f32[3,65536]{1,0:T(4,128)}, u32[]{:S(2)}) copy-start(f32[3,65536]{1,0:T(4,128)} %param.22) | copy-start | bytes 2359300
  663.0 10.1 %copy-start.1 = (f32[2,262144]{1,0:T(2,128)S(1)}, f32[2,262144]{1,0:T(2,128)}, u32[]{:S(2)}) copy-start(f32[2,262144]{1,0:T(2,128)} %param.27) | copy-start | bytes 6291460
Sparse Core Ops, SparseCore 0:
  403.8 51.8 all-reduce.1
where the time goes:
time: 739 us; the launch traced here: 726 us
  matrix products  279 us (38%)
  local copies, waits for them, and re-layouts  163 us (22%)
  other arithmetic  126 us (17%)
  blocking collectives  86.9 us (12%)
  waiting for transfers between devices  52.1 us (7%)
  between operations  17.1 us (2%)
    dot_general x16, matrix products, add_turn(): jnp.einsum('rgt,gpt->rgp', values.reshape(3, per_turn, TILE), tile_onehot...  120 us
    dot_general x16, matrix products, fetch(): jnp.einsum('rgp,gpt->rgt', slabs, tile_onehot(local_ids, per_turn, PB), p...  85.7 us
    psum x1, waiting for transfers between devices, on_device(): summed = lax.psum(reduced, 'cam')  52 us
    dot_general x16, matrix products, lookup(): jnp.einsum('rgc,gct->rgt', slabs, tile_onehot(cam_local, per_turn, CB), p...  47.6 us
    psum x1, blocking collectives, on_device(): cost_sum = lax.psum(jnp.sum(residual * residual), ('pts', 'cam'))  40.1 us
    dynamic_update_slice x16, local copies, waits for them, and re-layouts, lookup(): lax.dynamic_update_slice_in_dim(gathered, values.reshape(18, per_turn * T...  20.2 us
    reduce_sum x1, other arithmetic, couple(): first_row = jnp.sum(cam_rows[0:9] * cam_steps, axis=0)  19.1 us
    while x32, local copies, waits for them, and re-layouts  17.5 us
  transfers between devices with their start and end apart: 1, of which 1 were waited for; matrix products, arithmetic and copies ran while one was open for 0% of the time, Pallas kernels for 0%

commit v1 on v0

v1 whole, which is shorter than its diff:
```python
import functools
import math

import jax
import jax.numpy as jnp
from jax import lax
from jax.experimental import pallas as pl
from jax.experimental.pallas import tpu as pltpu
from jax.sharding import PartitionSpec as P

CB = 128
PB = 256
TILE = 256
UNIT = 8
HI = 8
LO = 32
PITCH = 24


def lanes(table, index):
    return jnp.take_along_axis(table, index, axis=1, mode="promise_in_bounds")


def reduce_kernel(
    units, tb_ref, tp_ref, tab_ref, cj_ref, pj_ref, cam_ref, pt_ref, out_ref, acc, s1, t1, v1
):
    step = pl.program_id(0)
    steps = pl.num_programs(0)

    @pl.when(step == 0)
    def _():
        acc[...] = jnp.zeros_like(acc)

    iota8 = lax.broadcasted_iota(jnp.int32, (8, 128), 0)

    def unit(u, carry):
        first_tile = step * (units * UNIT) + u * UNIT
        span = UNIT * TILE
        cols = pl.ds(pl.multiple_of(u * span, span), span)
        cj = cj_ref[:, cols].astype(jnp.float32)
        pj = pj_ref[:, cols].astype(jnp.float32)
        for c in range(2 * UNIT):
            piece = slice(c * 128, c * 128 + 128)
            row = ((c % 2) * UNIT + c // 2) * PITCH
            s1[row : row + 18, :] = cj[:, piece]
            s1[row + 18 : row + 24, :] = pj[:, piece]
        for s in range(UNIT):
            b = tb_ref[first_tile + s]
            t1[pl.ds(s, 8, stride=8), :] = tab_ref[b, 0:8, :]
            t1[64 + s : 65 + s, :] = tab_ref[b, 8:9, :]
        for half in range(2):
            def dense(r):
                return s1[pl.ds(half * UNIT * PITCH + r, UNIT, stride=PITCH), :]

            ids = cam_ref[pl.ds(u * 16 + half, UNIT, stride=2), :]
            first = second = None
            for m in range(9):
                g = lanes(t1[m * 8 : m * 8 + 8, :], ids)
                a, b2 = dense(m) * g, dense(9 + m) * g
                first = a if first is None else first + a
                second = b2 if second is None else second + b2
            for n in range(3):
                value = dense(18 + n) * first + dense(21 + n) * second
                big = value.astype(jnp.bfloat16).astype(jnp.float32)
                row = (half * 6 + n) * 8
                v1[row : row + 8, :] = big
                v1[row + 24 : row + 32, :] = value - big
        for s in range(UNIT):
            left, right = [], []
            for half in range(2):
                ids = pt_ref[pl.ds(u * 16 + 2 * s + half, 8, stride=0), :]
                inside = (ids >> 5) == iota8
                low = ids & 31
                left.append(
                    jnp.concatenate(
                        [
                            jnp.where(inside, v1[pl.ds((half * 6 + r) * 8 + s, 8, stride=0), :], 0.0)
                            for r in range(6)
                        ],
                        axis=0,
                    )
                )
                right.append(
                    jnp.concatenate(
                        [jnp.where(low == iota8 + 8 * j, 1.0, 0.0) for j in range(4)], axis=0
                    )
                )
            both = lax.dot_general(
                jnp.concatenate(left, axis=1).astype(jnp.bfloat16),
                jnp.concatenate(right, axis=1).astype(jnp.bfloat16),
                (((1,), (1,)), ((), ())),
                preferred_element_type=jnp.float32,
            )
            p = tp_ref[first_tile + s]
            acc[p, :, 0:LO] += both[0:24] + both[24:48]
        return carry

    lax.fori_loop(0, units, unit, 0)

    @pl.when(step == steps - 1)
    def _():
        lane = lax.broadcasted_iota(jnp.int32, (8, 128), 1)
        mine = (lane >> 5) == (iota8 & 3)

        def block(g, carry):
            for j in range(4):
                for n in range(3):
                    v = acc[g * 4 + j, n * 8 : n * 8 + 8, :]
                    v = v + pltpu.roll(v, 32, 1)
                    v = v + pltpu.roll(v, 64, 1)
                    v = jnp.where(mine, v, 0.0)
                    v = v + pltpu.roll(v, 1, 0)
                    v = v + pltpu.roll(v, 2, 0)
                    t1[j * 2 + n * 8 : j * 2 + n * 8 + 1, :] = v[3:4]
                    t1[j * 2 + n * 8 + 1 : j * 2 + n * 8 + 2, :] = v[7:8]
            for n in range(3):
                out_ref[n, pl.ds(pl.multiple_of(g * 8, 8), 8), :] = t1[n * 8 : n * 8 + 8, :]
            return carry

        lax.fori_loop(0, acc.shape[0] // 4, block, 0)


def project_kernel(
    units, tb_ref, tp_ref, tab_ref, pts_ref, obs_ref, cam_ref, pt_ref, res_ref, cost_ref, ptab, t1, t2
):
    step = pl.program_id(0)

    @pl.when(step == 0)
    def _():
        cost_ref[...] = jnp.zeros_like(cost_ref)
        quarter = pts_ref.shape[2]
        per = quarter // 16

        def fill(g, carry):
            src = g // per
            c = (g % per) * 16
            for n in range(3):
                for lh in range(2):
                    rows = pts_ref[src, n, pl.ds(c + lh, 8, stride=2), :]
                    ptab[pl.ds(g * 64 + n * 2 + lh, 8, stride=8), :] = rows
            return carry

        lax.fori_loop(0, pts_ref.shape[0] * per, fill, 0)

    def unit(u, total):
        first_tile = step * (units * UNIT) + u * UNIT
        for s in range(UNIT):
            b = tb_ref[first_tile + s]
            t1[pl.ds(s, 8, stride=8), :] = tab_ref[b, 0:8, :]
            t1[pl.ds(64 + s, 8, stride=8), :] = tab_ref[b, 8:16, :]
            p = tp_ref[first_tile + s]
            t2[pl.ds(s, 8, stride=8), :] = ptab[pl.ds(pl.multiple_of(p * 8, 8), 8), :]
        for half in range(2):
            ids = cam_ref[pl.ds(u * 16 + half, UNIT, stride=2), :]
            pid = pt_ref[pl.ds(u * 16 + half, UNIT, stride=2), :]
            low = pid & 127
            upper = pid >= 128
            x = [
                jnp.where(
                    upper,
                    lanes(t2[n * 16 + 8 : n * 16 + 16, :], low),
                    lanes(t2[n * 16 : n * 16 + 8, :], low),
                )
                for n in range(3)
            ]
            q = [lanes(t1[m * 8 : m * 8 + 8, :], ids) for m in range(15)]
            placed = [
                q[3 * n] * x[0] + q[3 * n + 1] * x[1] + q[3 * n + 2] * x[2] + q[9 + n]
                for n in range(3)
            ]
            depth = jnp.maximum(-placed[2], 1.0)
            px, py = placed[0] / depth, placed[1] / depth
            radius = px * px + py * py
            factor = q[12] * (1.0 + q[13] * radius + q[14] * radius * radius)
            for r, plane in ((0, px), (1, py)):
                where = pl.ds(u * 32 + 2 * half + r, UNIT, stride=4)
                res = factor * plane - obs_ref[where, :]
                res_ref[where, :] = res
                total = total + res * res
        return total

    total = lax.fori_loop(0, units, unit, jnp.zeros((8, 128), jnp.float32))
    cost_ref[...] += total


def camera_rows(cameras, increment):
    trial = cameras + increment
    w = trial[0:3]
    size = jnp.sqrt(jnp.sum(w * w, axis=0))
    cosine = jnp.cos(size)
    s1 = jnp.sinc(size / math.pi)
    s2 = 0.5 * jnp.square(jnp.sinc(size / (2.0 * math.pi)))
    rows = [
        cosine + s2 * w[0] * w[0],
        s2 * w[0] * w[1] - s1 * w[2],
        s2 * w[0] * w[2] + s1 * w[1],
        s2 * w[1] * w[0] + s1 * w[2],
        cosine + s2 * w[1] * w[1],
        s2 * w[1] * w[2] - s1 * w[0],
        s2 * w[2] * w[0] - s1 * w[1],
        s2 * w[2] * w[1] + s1 * w[0],
        cosine + s2 * w[2] * w[2],
    ]
    return jnp.concatenate([jnp.stack(rows), trial[3:9], increment], axis=0)


def spread(value, axis, size):
    parts = [value]
    for s in range(1, size):
        parts.append(lax.ppermute(value, axis, [(k, (k + s) % size) for k in range(size)]))
    return jnp.stack(parts)


def on_device(
    n_pts,
    n_cam,
    cameras,
    increment,
    points,
    point_gradient,
    point_inverse,
    cam_jacobian,
    point_jacobian,
    observed,
    tile_block,
    tile_points,
    obs_camera,
    obs_point,
    accept,
):
    both = ("pts", "cam")
    mine = camera_rows(cameras, increment)
    table = lax.all_to_all(
        jnp.broadcast_to(mine[None], (n_pts * n_cam,) + mine.shape), both, 0, 0
    )
    blocks = table.shape[0] * table.shape[2] // CB
    table = table.reshape(table.shape[0], 24, -1, CB).transpose(0, 2, 1, 3).reshape(blocks, 24, CB)
    rot_table = jnp.pad(table[:, 0:15], ((0, 0), (0, 1), (0, 0)))
    inc_table = jnp.pad(table[:, 15:24], ((0, 0), (0, 7), (0, 0)))

    tiles = tile_block.shape[0]
    count = obs_camera.shape[0]
    point_count = points.shape[1]
    point_blocks = point_count // PB
    ids_cam = obs_camera.reshape(-1, 128)
    ids_pt = obs_point.reshape(-1, 128)
    steps = math.gcd(tiles // UNIT, 16)
    units = tiles // (UNIT * steps)
    obs_step = count // steps

    reduced = pl.pallas_call(
        functools.partial(reduce_kernel, units),
        out_shape=jax.ShapeDtypeStruct((3, point_count // 128, 128), jnp.float32),
        grid_spec=pltpu.PrefetchScalarGridSpec(
            num_scalar_prefetch=2,
            grid=(steps,),
            in_specs=[
                pl.BlockSpec((blocks, 16, CB), lambda i, a, b: (0, 0, 0)),
                pl.BlockSpec((18, obs_step), lambda i, a, b: (0, i)),
                pl.BlockSpec((6, obs_step), lambda i, a, b: (0, i)),
                pl.BlockSpec((obs_step // 128, 128), lambda i, a, b: (i, 0)),
                pl.BlockSpec((obs_step // 128, 128), lambda i, a, b: (i, 0)),
            ],
            out_specs=pl.BlockSpec((3, point_count // 128, 128), lambda i, a, b: (0, 0, 0)),
            scratch_shapes=[
                pltpu.VMEM((point_blocks, 24, 128), jnp.float32),
                pltpu.VMEM((2 * UNIT * PITCH, 128), jnp.float32),
                pltpu.VMEM((72, 128), jnp.float32),
                pltpu.VMEM((96, 128), jnp.float32),
            ],
        ),
        compiler_params=pltpu.CompilerParams(dimension_semantics=("arbitrary",)),
        name="reduce_points",
    )(tile_block, tile_points, inc_table, cam_jacobian, point_jacobian, ids_cam, ids_pt)

    me = lax.axis_index("cam")
    rows = point_count // 128 // n_cam
    parts = reduced.reshape(3, n_cam, rows, 128)
    summed = lax.dynamic_index_in_dim(parts, me, 1, False)
    for s in range(1, n_cam):
        piece = lax.dynamic_index_in_dim(parts, lax.rem(me + s, n_cam), 1, False)
        summed = summed + lax.ppermute(piece, "cam", [(k, (k + s) % n_cam) for k in range(n_cam)])

    def own(array):
        part = lax.dynamic_slice_in_dim(array, me * (rows * 128), rows * 128, 1)
        return part.reshape(array.shape[0], rows, 128)

    residue = own(point_gradient) - summed
    inverse = own(point_inverse)
    point_step = jnp.stack(
        [
            inverse[3 * i] * residue[0]
            + inverse[3 * i + 1] * residue[1]
            + inverse[3 * i + 2] * residue[2]
            for i in range(3)
        ]
    )
    trial = spread(own(points) + point_step, "cam", n_cam)
    trial = jnp.take(trial, jnp.mod(me - jnp.arange(n_cam), n_cam), axis=0)

    obs_rows = observed.reshape(2, -1, 128).transpose(1, 0, 2).reshape(-1, 128)
    residual, partial = pl.pallas_call(
        functools.partial(project_kernel, units),
        out_shape=(
            jax.ShapeDtypeStruct(obs_rows.shape, jnp.float32),
            jax.ShapeDtypeStruct((8, 128), jnp.float32),
        ),
        grid_spec=pltpu.PrefetchScalarGridSpec(
            num_scalar_prefetch=2,
            grid=(steps,),
            in_specs=[
                pl.BlockSpec((blocks, 16, CB), lambda i, a, b: (0, 0, 0)),
                pl.BlockSpec((n_cam, 3, rows, 128), lambda i, a, b: (0, 0, 0, 0)),
                pl.BlockSpec((obs_step // 64, 128), lambda i, a, b: (i, 0)),
                pl.BlockSpec((obs_step // 128, 128), lambda i, a, b: (i, 0)),
                pl.BlockSpec((obs_step // 128, 128), lambda i, a, b: (i, 0)),
            ],
            out_specs=(
                pl.BlockSpec((obs_step // 64, 128), lambda i, a, b: (i, 0)),
                pl.BlockSpec((8, 128), lambda i, a, b: (0, 0)),
            ),
            scratch_shapes=[
                pltpu.VMEM((point_blocks * 8, 128), jnp.float32),
                pltpu.VMEM((128, 128), jnp.float32),
                pltpu.VMEM((64, 128), jnp.float32),
            ],
        ),
        compiler_params=pltpu.CompilerParams(dimension_semantics=("arbitrary",)),
        name="project_points",
    )(tile_block, tile_points, rot_table, trial, obs_rows, ids_cam, ids_pt)
    residual = residual.reshape(-1, 2, 128).transpose(1, 0, 2).reshape(2, -1)

    partial = jnp.sum(partial, axis=0, keepdims=True)
    spread_sums = lax.all_to_all(
        jnp.broadcast_to(partial, (n_pts * n_cam, 128)), both, 0, 0
    )
    trial_cost = jnp.sum(spread_sums) / (2.0 * count * n_pts * n_cam)
    flag = jnp.remainder(accept, 2).astype(jnp.float32)
    trial_natural = trial.transpose(1, 0, 2, 3).reshape(3, point_count)
    accepted_points = jnp.where(flag > 0.0, trial_natural, points)
    return residual, trial_cost, accepted_points, cameras + flag * increment


def solution(mesh):
    in_specs = (
        P(None, ("pts", "cam")),
        P(None, ("pts", "cam")),
        P(None, "pts"),
        P(None, "pts"),
        P(None, "pts"),
        P(None, ("pts", "cam")),
        P(None, ("pts", "cam")),
        P(None, ("pts", "cam")),
        P(("pts", "cam")),
        P(("pts", "cam")),
        P(("pts", "cam")),
        P(("pts", "cam")),
        P(),
    )
    out_specs = (P(None, ("pts", "cam")), P(), P(None, "pts"), P(None, ("pts", "cam")))
    body = functools.partial(on_device, mesh.shape["pts"], mesh.shape["cam"])
    return jax.shard_map(body, mesh=mesh, in_specs=in_specs, out_specs=out_specs, check_vma=False)
```

time: 739 us -> 163 us (0.22); the launches traced: 726 us -> 163 us
  matrix products: 279 us -> 0 us
  local copies, waits for them, and re-layouts: 163 us -> 10.1 us
  other arithmetic: 126 us -> 7.53 us
  blocking collectives: 86.9 us -> 0 us
  Pallas kernels: 0 us -> 80.2 us
  starting transfers between devices: 0.04 us -> 25.9 us
  waiting for transfers between devices: 52.1 us -> 35.8 us
  between operations: 17.1 us -> 3.36 us
    dot_general x96 -> x0, matrix products: 279 us -> none  [the longest x16 120 us: add_turn(): jnp.einsum('rgt,gpt->rgp', values.reshape(3, per_turn, TILE), tile_onehot...]
    dynamic_slice x112 -> x0, local copies, waits for them, and re-layouts: 93.5 us -> none  [the longest x16 16.1 us: add_turn(): lax.dynamic_slice_in_dim(coupling, turn * per_turn * TILE, per_turn * TIL...]
    pallas_call x0 -> x2, Pallas kernels: none -> 80.2 us  [the longest x1 54.7 us: on_device(): pl.pallas_call(functools.partial(reduce_kernel, units), out_shape=jax.Sha...]
    psum x1 -> x0, waiting for transfers between devices: 52 us -> none  [on_device(): summed = lax.psum(reduced, 'cam')]
    all_gather x4 -> x0, blocking collectives: 46.8 us -> none  [the longest x1 15.1 us: on_device(): lax.all_gather(increment, 'cam', axis=1, tiled=True)]
    reduce_sum x4 -> x3, other arithmetic: 45.9 us -> 1.31 us  [the longest x1 0.69 us: on_device(): partial = jnp.sum(partial, axis=0, keepdims=True)]
    psum x1 -> x0, blocking collectives: 40.1 us -> none  [on_device(): cost_sum = lax.psum(jnp.sum(residual * residual), ('pts', 'cam'))]
    dynamic_update_slice x32 -> x0, local copies, waits for them, and re-layouts: 32.5 us -> none  [the longest x16 20.2 us: lookup(): lax.dynamic_update_slice_in_dim(gathered, values.reshape(18, per_turn * T...]
  transfers between devices with their start and end apart: 1 -> 8, of which waited for: 1 -> 6; matrix products, arithmetic and copies ran while one was open for 0% -> 5% of each run, Pallas kernels for 0% -> 0%
where the time goes in v1:
time: 163 us
  Pallas kernels  80.2 us (49%)
  waiting for transfers between devices  35.8 us (22%)
  starting transfers between devices  25.9 us (16%)
  local copies, waits for them, and re-layouts  10.1 us (6%)
  other arithmetic  7.53 us (5%)
  between operations  3.36 us (2%)
    pallas_call x1, Pallas kernels, on_device(): pl.pallas_call(functools.partial(reduce_kernel, units), out_shape=jax.Sha...  54.7 us
    pallas_call x1, Pallas kernels, on_device(): pl.pallas_call(functools.partial(project_kernel, units), out_shape=(jax.S...  25.4 us
    ppermute x3, waiting for transfers between devices, on_device(): lax.ppermute(piece, 'cam', [(k, (k + s) % n_cam) for k in range(n_cam)])  12.8 us
    ppermute x3, waiting for transfers between devices, spread(): lax.ppermute(value, axis, [(k, (k + s) % size) for k in range(size)])  11.2 us
    all_to_all x1, starting transfers between devices, on_device(): lax.all_to_all(jnp.broadcast_to(partial, (n_pts * n_cam, 128)), both, 0, 0)  7.38 us
    all_to_all x1, starting transfers between devices, on_device(): lax.all_to_all(jnp.broadcast_to(mine[None], (n_pts * n_cam,) + mine.shape...  7.33 us
    ppermute x3, starting transfers between devices, spread(): lax.ppermute(value, axis, [(k, (k + s) % size) for k in range(size)])  6.6 us
    all_to_all x1, waiting for transfers between devices, on_device(): lax.all_to_all(jnp.broadcast_to(mine[None], (n_pts * n_cam,) + mine.shape...  6.42 us
  transfers between devices with their start and end apart: 8, of which 6 were waited for; matrix products, arithmetic and copies ran while one was open for 5% of the time, Pallas kernels for 0%

profile of v1, /device:TPU:0, one launch (start us, length us, event | category | flops | bytes accessed | tf_op | source)
XLA Modules:
  0.0 162.9 jit_solution(7123387660319731507)
XLA Ops:
  0.6 0.0 copy-start
  1.4 1.3 multiply_add_fusion.3
  2.8 0.1 add_bitcast_fusion.1
  2.9 0.8 concatenate.10
  3.7 0.8 broadcast_in_dim.25
  4.4 7.3 %all-to-all-start = ((f32[32,24,128]{2,1,0:T(8,128)}), f32[32,24,128]{2,1,0:T(8,128)S(1)}, u32[]{:S(2)}, u32[]{:S(2)}) async-start(f32[32,24,128]{2,1,0:T(8,128)} %broadcast_in_dim.25), calls=%async_computation | async-start | bytes 786432 | tf_op jit(solution)/shard_map/all_to_all | solution.py:233
  11.8 4.3 %constant_dynamic-slice_fusion = (f32[1,16384]{1,0:T(1,128)S(1)}, f32[1,16384]{1,0:T(1,128)S(1)}, f32[1,16384]{1,0:T(1,128)S(1)}, f32[1,16384]{1,0:T(1,128)S(1)}...) fusion(f32[9,65536]{1,0:T(8,128)} %param.18, ...), kind=kLoop, calls=%fused_computation.38 | loop fusion | bytes 1179684 | tf_op jit(solution)/shard_map/slice | solution.py:292
  16.1 0.0 copy-done
  16.1 0.1 dynamic-slice_bitcast_fusion
  16.2 1.0 dynamic-slice_bitcast_fusion.1
  17.2 6.4 %all-to-all-done = f32[32,24,128]{2,1,0:T(8,128)S(1)} async-done(((f32[32,24,128]{2,1,0:T(8,128)}), f32[32,24,128]{2,1,0:T(8,128)S(1)}, u32[]{:S(2)}, u32[]{:S(2)}) %all-to-all-start) | async-done | bytes 393248 | tf_op jit(solution)/shard_map/all_to_all | solution.py:233
  23.7 0.7 pad.9.tab_ref
  24.4 0.0 copy-start.2
  24.4 54.7 %reduce_points.1 = f32[3,512,128]{2,1,0:T(8,128)} custom-call(s32[1024]{0:T(1024)} %tb_ref.3, s32[1024]{0:T(1024)} %tp_ref.3, f32[32,16,128]{2,1,0:T(8,128)} %pad.9.tab_ref, bf16[18,262144]{1,0:T(8,128)(2,1)} %cj_ref.1, bf16[6,262144]{1,0:T(8,128)(2,1)} %pj_ref.1, s32[2048,128]{1,0:T(8,128)} %bitcast.129, s32[2048,128]{1,0:T(8,128)} %bitcast.131), custom_call_target="tpu_custom_call" | custom-call | tf_op jit(solution)/shard_map/reduce_points/pallas_call | solution.py:251
  79.1 1.2 dynamic-slice_bitcast_fusion.4
  80.3 2.2 %collective-permute-start = (f32[3,128,128]{2,1,0:T(8,128)S(1)}, f32[3,128,128]{2,1,0:T(8,128)S(1)}, u32[]{:S(2)}, u32[]{:S(2)}) collective-permute-start(f32[3,128,128]{2,1,0:T(8,128)S(1)} %get-tuple-element.22), channel_id=1, source_target_pairs={{0,1},{1,2},{2,3},{3,0},{4,5},{5,6},{6,7},{7,4},{8,9},{9,10},{10,1... | collective-permute-start | bytes 589832 | tf_op jit(solution)/shard_map/ppermute | solution.py:282
  82.5 1.0 collective-permute-start.1
  83.4 1.5 collective-permute-start.2
  84.9 0.0 copy-done.2
  84.9 0.8 slice_select_fusion.tab_ref
  85.7 4.1 %collective-permute-done = f32[3,128,128]{2,1,0:T(8,128)S(1)} collective-permute-done((f32[3,128,128]{2,1,0:T(8,128)S(1)}, f32[3,128,128]{2,1,0:T(8,128)S(1)}, u32[]{:S(2)}, u32[]{:S(2)}) %collective-permute-start) | collective-permute-done | bytes 196640 | tf_op jit(solution)/shard_map/ppermute | solution.py:282
  89.9 8.6 %collective-permute-done.1 = f32[3,128,128]{2,1,0:T(8,128)S(1)} collective-permute-done((f32[3,128,128]{2,1,0:T(8,128)S(1)}, f32[3,128,128]{2,1,0:T(8,128)S(1)}, u32[]{:S(2)}, u32[]{:S(2)}) %collective-permute-start.1) | collective-permute-done | bytes 196640 | tf_op jit(solution)/shard_map/ppermute | solution.py:282
  98.5 0.0 collective-permute-done.2
  98.5 1.0 bitcast_subtract_fusion
  99.6 4.2 %collective-permute-start.3 = (f32[3,128,128]{2,1,0:T(8,128)S(1)}, f32[3,128,128]{2,1,0:T(8,128)S(1)}, u32[]{:S(2)}, u32[]{:S(2)}) collective-permute-start(f32[3,128,128]{2,1,0:T(8,128)S(1)} %bitcast_add_fusion), channel_id=1, source_target_pairs={{0,1},{1,2},{2,3},{3,0},{4,5},{5,6},{6,7},{7,4},{8,9},{9,10},{10,1... | collective-permute-start | bytes 589832 | tf_op jit(solution)/shard_map/ppermute | solution.py:210
  103.7 0.9 collective-permute-start.4
  104.6 1.6 collective-permute-start.5
  106.2 3.7 %collective-permute-done.3 = f32[3,128,128]{2,1,0:T(8,128)S(1)} collective-permute-done((f32[3,128,128]{2,1,0:T(8,128)S(1)}, f32[3,128,128]{2,1,0:T(8,128)S(1)}, u32[]{:S(2)}, u32[]{:S(2)}) %collective-permute-start.3) | collective-permute-done | bytes 196640 | tf_op jit(solution)/shard_map/ppermute | solution.py:210
  109.9 7.5 %collective-permute-done.4 = f32[3,128,128]{2,1,0:T(8,128)S(1)} collective-permute-done((f32[3,128,128]{2,1,0:T(8,128)S(1)}, f32[3,128,128]{2,1,0:T(8,128)S(1)}, u32[]{:S(2)}, u32[]{:S(2)}) %collective-permute-start.4) | collective-permute-done | bytes 196640 | tf_op jit(solution)/shard_map/ppermute | solution.py:210
  117.4 0.0 collective-permute-done.5
  117.4 0.1 pad_maximum_fusion
  117.4 0.6 gather_fusion
  118.0 1.0 broadcast_select_fusion.pts_ref
  119.1 0.1 fusion.17
  119.2 0.0 copy-start.1
  119.2 25.4 %project_points.1 = (f32[4096,128]{1,0:T(8,128)}, f32[8,128]{1,0:T(8,128)}) custom-call(s32[1024]{0:T(1024)} %tb_ref.3, s32[1024]{0:T(1024)} %tp_ref.3, f32[32,16,128]{2,1,0:T(8,128)} %slice_select_fusion.tab_ref, f32[4,3,128,128]{3,2,1,0:T(8,128)} %broadcast_select_fusion.pts_ref, f32[4096,128]{1,0:T(8,128)} %bitcast.136, s32[2048,128]{1,0:T(8,128)} %bitcast.130, ...), custom_call_target="tpu_custom_call" | custom-call | tf_op jit(solution)/shard_map/project_points/pallas_call | solution.py:302
  144.6 0.7 reduce_sum.28
  145.3 0.6 broadcast_in_dim.28
  145.9 7.4 %all-to-all-start.1 = ((f32[32,1,128]{2,1,0:T(1,128)}), f32[32,1,128]{2,1,0:T(1,128)S(1)}, u32[]{:S(2)}, u32[]{:S(2)}) async-start(f32[32,1,128]{2,1,0:T(1,128)} %broadcast_in_dim.28), calls=%async_computation.1 | async-start | bytes 32768 | tf_op jit(solution)/shard_map/all_to_all | solution.py:334
  153.3 0.1 copy.28
  153.4 0.0 copy-done.1
  153.4 1.7 %bitcast_select_fusion = f32[3,65536]{1,0:T(4,128)} fusion(f32[3,65536]{1,0:T(4,128)S(1)} %copy-done.1, f32[1,3,512,128]{3,2,1,0:T(8,128)S(1)} %bitcast.135, pred[]{:T(512)S(6)} %gt.3), kind=kLoop, calls=%fused_computation.1 | loop fusion | flops 196608 | bytes 2359297 | tf_op jit(solution)/shard_map/jit(_where)/select_n | solution.py:340
  155.1 5.5 %all-to-all-done.1 = f32[32,1,128]{2,1,0:T(1,128)S(1)} async-done(((f32[32,1,128]{2,1,0:T(1,128)}), f32[32,1,128]{2,1,0:T(1,128)S(1)}, u32[]{:S(2)}, u32[]{:S(2)}) %all-to-all-start.1) | async-done | bytes 16416 | tf_op jit(solution)/shard_map/all_to_all | solution.py:334
  160.5 0.6 reduce_sum.29
  (11 shorter events, 0.2 us)
Async XLA Ops:
  0.6 15.5 %copy-start = (f32[3,65536]{1,0:T(4,128)S(1)}, f32[3,65536]{1,0:T(4,128)}, u32[]{:S(2)}) copy-start(f32[3,65536]{1,0:T(4,128)} %param.17) | copy-start | bytes 2359300
  4.4 19.2 %all-to-all-start = ((f32[32,24,128]{2,1,0:T(8,128)}), f32[32,24,128]{2,1,0:T(8,128)S(1)}, u32[]{:S(2)}, u32[]{:S(2)}) async-start(f32[32,24,128]{2,1,0:T(8,128)} %broadcast_in_dim.25), calls=%async_computation | async-start | bytes 786432 | tf_op jit(solution)/shard_map/all_to_all | solution.py:233
  24.4 60.5 %copy-start.2 = (pred[16]{0:T(512)(128)(4,1)S(1)}, pred[16]{0:T(512)(128)(4,1)}, u32[]{:S(2)}) copy-start(pred[16]{0:T(512)(128)(4,1)} %constant.96.clone.1) | copy-start | bytes 52
  80.3 9.6 %collective-permute-start = (f32[3,128,128]{2,1,0:T(8,128)S(1)}, f32[3,128,128]{2,1,0:T(8,128)S(1)}, u32[]{:S(2)}, u32[]{:S(2)}) collective-permute-start(f32[3,128,128]{2,1,0:T(8,128)S(1)} %get-tuple-element.22), channel_id=1, source_target_pairs={{0,1},{1,2},{2,3},{3,0},{4,5},{5,6},{6,7},{7,4},{8,9},{9,10},{10,1... | collective-permute-start | bytes 589832 | tf_op jit(solution)/shard_map/ppermute | solution.py:282
  82.5 16.0 %collective-permute-start.1 = (f32[3,128,128]{2,1,0:T(8,128)S(1)}, f32[3,128,128]{2,1,0:T(8,128)S(1)}, u32[]{:S(2)}, u32[]{:S(2)}) collective-permute-start(f32[3,128,128]{2,1,0:T(8,128)S(1)} %get-tuple-element.24), channel_id=1, source_target_pairs={{0,2},{1,3},{2,0},{3,1},{4,6},{5,7},{6,4},{7,5},{8,10},{9,11},{10,... | collective-permute-start | bytes 589832 | tf_op jit(solution)/shard_map/ppermute | solution.py:282
  83.4 15.0 %collective-permute-start.2 = (f32[3,128,128]{2,1,0:T(8,128)S(1)}, f32[3,128,128]{2,1,0:T(8,128)S(1)}, u32[]{:S(2)}, u32[]{:S(2)}) collective-permute-start(f32[3,128,128]{2,1,0:T(8,128)S(1)} %get-tuple-element.23), channel_id=1, source_target_pairs={{0,3},{1,0},{2,1},{3,2},{4,7},{5,4},{6,5},{7,6},{8,11},{9,8},{10,9... | collective-permute-start | bytes 589832 | tf_op jit(solution)/shard_map/ppermute | solution.py:282
  99.6 10.3 %collective-permute-start.3 = (f32[3,128,128]{2,1,0:T(8,128)S(1)}, f32[3,128,128]{2,1,0:T(8,128)S(1)}, u32[]{:S(2)}, u32[]{:S(2)}) collective-permute-start(f32[3,128,128]{2,1,0:T(8,128)S(1)} %bitcast_add_fusion), channel_id=1, source_target_pairs={{0,1},{1,2},{2,3},{3,0},{4,5},{5,6},{6,7},{7,4},{8,9},{9,10},{10,1... | collective-permute-start | bytes 589832 | tf_op jit(solution)/shard_map/ppermute | solution.py:210
  103.7 13.6 %collective-permute-start.4 = (f32[3,128,128]{2,1,0:T(8,128)S(1)}, f32[3,128,128]{2,1,0:T(8,128)S(1)}, u32[]{:S(2)}, u32[]{:S(2)}) collective-permute-start(f32[3,128,128]{2,1,0:T(8,128)S(1)} %bitcast_add_fusion), channel_id=1, source_target_pairs={{0,2},{1,3},{2,0},{3,1},{4,6},{5,7},{6,4},{7,5},{8,10},{9,11},{10,... | collective-permute-start | bytes 589832 | tf_op jit(solution)/shard_map/ppermute | solution.py:210
  104.6 12.8 %collective-permute-start.5 = (f32[3,128,128]{2,1,0:T(8,128)S(1)}, f32[3,128,128]{2,1,0:T(8,128)S(1)}, u32[]{:S(2)}, u32[]{:S(2)}) collective-permute-start(f32[3,128,128]{2,1,0:T(8,128)S(1)} %bitcast_add_fusion), channel_id=1, source_target_pairs={{0,3},{1,0},{2,1},{3,2},{4,7},{5,4},{6,5},{7,6},{8,11},{9,8},{10,9... | collective-permute-start | bytes 589832 | tf_op jit(solution)/shard_map/ppermute | solution.py:210
  119.2 34.2 %copy-start.1 = (f32[3,65536]{1,0:T(4,128)S(1)}, f32[3,65536]{1,0:T(4,128)}, u32[]{:S(2)}) copy-start(f32[3,65536]{1,0:T(4,128)} %param.16) | copy-start | bytes 2359300
  145.9 14.6 %all-to-all-start.1 = ((f32[32,1,128]{2,1,0:T(1,128)}), f32[32,1,128]{2,1,0:T(1,128)S(1)}, u32[]{:S(2)}, u32[]{:S(2)}) async-start(f32[32,1,128]{2,1,0:T(1,128)} %broadcast_in_dim.28), calls=%async_computation.1 | async-start | bytes 32768 | tf_op jit(solution)/shard_map/all_to_all | solution.py:334

commit v2 on v1

v2 whole, which is shorter than its diff:
```python
import functools
import math

import jax
import jax.numpy as jnp
from jax import lax
from jax.experimental import pallas as pl
from jax.experimental.pallas import tpu as pltpu
from jax.sharding import PartitionSpec as P

CB = 128
PB = 256
TILE = 256
UNIT = 8
HI = 8
LO = 32
PITCH = 28
WAYS = 16
WAYS2 = 16
CHUNKS = 8
GATHER = 16
AHEAD = 2


def lanes(table, index):
    return jnp.take_along_axis(table, index, axis=1, mode="promise_in_bounds")


def arrivals(chunks, pairs, sems):
    def copies(c):
        out = []
        for k, (src, dst, axis) in enumerate(pairs):
            size = src.shape[axis] // chunks
            piece = pl.ds(pl.multiple_of(c * size, size), size)
            where = (slice(None), piece) if axis else (piece, slice(None))
            out.append(pltpu.make_async_copy(src.at[where], dst.at[where], sems.at[c, k]))
        return out

    def start(c):
        @pl.when(c < chunks)
        def _():
            for copy in copies(c):
                copy.start()

    def wait(c):
        for copy in copies(c):
            copy.wait()

    return start, wait


def reduce_kernel(
    n_cam, me_ref, tb_ref, tp_ref, tab_ref, cj_hbm, pj_hbm, cam_hbm, pt_hbm, *refs
):
    out_refs, refs = refs[:n_cam], refs[n_cam:]
    reduce_body(
        me_ref, tb_ref, tp_ref, tab_ref, cj_hbm, pj_hbm, cam_hbm, pt_hbm, out_refs, *refs
    )


def reduce_body(
    me_ref, tb_ref, tp_ref, tab_ref, cj_hbm, pj_hbm, cam_hbm, pt_hbm, out_refs,
    cj_ref, pj_ref, cam_ref, pt_ref, sems, fin, acc, *scratch
):
    s1s = scratch[:WAYS]
    t1s = scratch[WAYS : 2 * WAYS]
    v1s = scratch[2 * WAYS : 3 * WAYS]
    chunks = sems.shape[0]
    trips = cam_ref.shape[0] // (2 * UNIT * WAYS * chunks)
    start, wait = arrivals(
        chunks,
        ((cj_hbm, cj_ref, 1), (pj_hbm, pj_ref, 1), (cam_hbm, cam_ref, 0), (pt_hbm, pt_ref, 0)),
        sems,
    )
    for c in range(AHEAD):
        start(c)
    acc[...] = jnp.zeros_like(acc)

    iota8 = lax.broadcasted_iota(jnp.int32, (8, 128), 0)

    def couple(u, s1, t1, v1):
        first_tile = u * UNIT
        span = UNIT * TILE
        cols = pl.ds(pl.multiple_of(u * span, span), span)
        cj = cj_ref[:, cols].astype(jnp.float32)
        pj = pj_ref[:, cols].astype(jnp.float32)
        for c in range(2 * UNIT):
            piece = slice(c * 128, c * 128 + 128)
            row = ((c % 2) * UNIT + c // 2) * PITCH
            s1[row : row + 18, :] = cj[:, piece]
            s1[row + 18 : row + 24, :] = pj[:, piece]
        for s in range(UNIT):
            b = tb_ref[first_tile + s]
            t1[pl.ds(s, 8, stride=9), :] = tab_ref[b, 0:8, :]
            t1[72 + s : 73 + s, :] = tab_ref[b, 8:9, :]
        for half in range(2):

            def dense(r):
                return s1[pl.ds(half * UNIT * PITCH + r, UNIT, stride=PITCH), :]

            ids = cam_ref[pl.ds(u * 16 + half, UNIT, stride=2), :]
            first = second = None
            for m in range(9):
                g = lanes(t1[m * 9 : m * 9 + 8, :], ids)
                a, b2 = dense(m) * g, dense(9 + m) * g
                first = a if first is None else first + a
                second = b2 if second is None else second + b2
            for n in range(3):
                value = dense(18 + n) * first + dense(21 + n) * second
                big = value.astype(jnp.bfloat16).astype(jnp.float32)
                row = (half * 6 + n) * 8
                v1[row : row + 8, :] = big
                v1[row + 24 : row + 32, :] = value - big

    def products(u, v1):
        sums = []
        for s in range(UNIT):
            left, right = [], []
            for half in range(2):
                ids = pt_ref[pl.ds(u * 16 + 2 * s + half, 8, stride=0), :]
                inside = (ids >> 5) == iota8
                low = ids & 31
                left.append(
                    jnp.concatenate(
                        [
                            jnp.where(inside, v1[pl.ds((half * 6 + r) * 8 + s, 8, stride=0), :], 0.0)
                            for r in range(6)
                        ],
                        axis=0,
                    )
                )
                right.append(
                    jnp.concatenate(
                        [jnp.where(low == iota8 + 8 * j, 1.0, 0.0) for j in range(4)], axis=0
                    )
                )
            both = lax.dot_general(
                jnp.concatenate(left, axis=1).astype(jnp.bfloat16),
                jnp.concatenate(right, axis=1).astype(jnp.bfloat16),
                (((1,), (1,)), ((), ())),
                preferred_element_type=jnp.float32,
            )
            sums.append(both[0:24] + both[24:48])
        return sums

    def store(u, sums):
        for s in range(0, UNIT, 2):
            p0, p1 = tp_ref[u * UNIT + s], tp_ref[u * UNIT + s + 1]
            old0, old1 = acc[p0, :, 0:LO], acc[p1, :, 0:LO]
            acc[p0, :, 0:LO] = old0 + sums[s]
            acc[p1, :, 0:LO] = old1 + (sums[s + 1] + jnp.where(p0 == p1, sums[s], 0.0))

    def chunk(c, carry):
        start(c + AHEAD)
        wait(c)

        def trip(i, carry):
            first = (c * trips + i) * WAYS
            for w in range(WAYS):
                couple(first + w, s1s[w], t1s[w], v1s[w])
            for w in range(WAYS):
                store(first + w, products(first + w, v1s[w]))
            return carry

        return lax.fori_loop(0, trips, trip, carry)

    lax.fori_loop(0, chunks, chunk, 0)

    lane = lax.broadcasted_iota(jnp.int32, (8, 128), 1)
    mine = (lane >> 5) == (iota8 & 3)
    groups = out_refs[0].shape[1] // 8
    gather = math.gcd(groups, GATHER)

    for slot, out_ref in enumerate(out_refs):
        base = lax.rem(me_ref[0] + slot, len(out_refs)) * groups

        def part(i, carry, out_ref=out_ref, base=base):
            for g in range(gather):
                for j in range(4):
                    for n in range(3):
                        b = (base + i * gather + g) * 4 + j
                        v = acc[b, n * 8 : n * 8 + 8, :]
                        v = v + pltpu.roll(v, 32, 1)
                        v = v + pltpu.roll(v, 64, 1)
                        v = jnp.where(mine, v, 0.0)
                        v = v + pltpu.roll(v, 1, 0)
                        v = v + pltpu.roll(v, 2, 0)
                        row = g * 24 + n * 8 + j * 2
                        fin[row : row + 1, :] = v[3:4]
                        fin[row + 1 : row + 2, :] = v[7:8]
            for g in range(gather):
                rows = pl.ds(pl.multiple_of((i * gather + g) * 8, 8), 8)
                for n in range(3):
                    out_ref[n, rows, :] = fin[g * 24 + n * 8 : g * 24 + n * 8 + 8, :]
            return carry

        lax.fori_loop(0, groups // gather, part, 0)


def project_kernel(
    n_cam, me_ref, tb_ref, tp_ref, tab_ref, *refs
):
    project_body(me_ref, tb_ref, tp_ref, tab_ref, refs[:n_cam], *refs[n_cam:])


def project_body(
    me_ref, tb_ref, tp_ref, tab_ref, pts_refs, obs_hbm, cam_hbm, pt_hbm, res_hbm, cost_ref,
    obs_ref, cam_ref, pt_ref, res_ref, sems, out_sems, ptab, *scratch
):
    t1s, t2s = scratch[:WAYS2], scratch[WAYS2:]
    chunks = sems.shape[0]
    trips = cam_ref.shape[0] // (2 * UNIT * WAYS2 * chunks)
    start, wait = arrivals(
        chunks, ((obs_hbm, obs_ref, 0), (cam_hbm, cam_ref, 0), (pt_hbm, pt_ref, 0)), sems
    )
    for c in range(AHEAD):
        start(c)
    per = pts_refs[0].shape[1] // 16
    for slot, pts_ref in enumerate(pts_refs):
        base = lax.rem(me_ref[0] + len(pts_refs) - slot, len(pts_refs)) * per

        def fill(g, carry, pts_ref=pts_ref, base=base):
            for n in range(3):
                for lh in range(2):
                    rows = pts_ref[n, pl.ds(g * 16 + lh, 8, stride=2), :]
                    ptab[pl.ds((base + g) * 64 + n * 2 + lh, 8, stride=8), :] = rows
            return carry

        lax.fori_loop(0, per, fill, 0)

    def project(u, t1, t2, total):
        first_tile = u * UNIT
        for s in range(UNIT):
            b = tb_ref[first_tile + s]
            t1[pl.ds(s, 8, stride=9), :] = tab_ref[b, 0:8, :]
            t1[pl.ds(72 + s, 8, stride=9), :] = tab_ref[b, 8:16, :]
            p = tp_ref[first_tile + s]
            t2[pl.ds(s, 8, stride=9), :] = ptab[pl.ds(pl.multiple_of(p * 8, 8), 8), :]
        for half in range(2):
            ids = cam_ref[pl.ds(u * 16 + half, UNIT, stride=2), :]
            pid = pt_ref[pl.ds(u * 16 + half, UNIT, stride=2), :]
            low = pid & 127
            upper = pid >= 128
            x = [
                jnp.where(
                    upper,
                    lanes(t2[n * 18 + 9 : n * 18 + 17, :], low),
                    lanes(t2[n * 18 : n * 18 + 8, :], low),
                )
                for n in range(3)
            ]
            q = [lanes(t1[m * 9 : m * 9 + 8, :], ids) for m in range(15)]
            placed = [
                q[3 * n] * x[0] + q[3 * n + 1] * x[1] + q[3 * n + 2] * x[2] + q[9 + n]
                for n in range(3)
            ]
            depth = jnp.maximum(-placed[2], 1.0)
            px, py = placed[0] / depth, placed[1] / depth
            radius = px * px + py * py
            factor = q[12] * (1.0 + q[13] * radius + q[14] * radius * radius)
            for r, plane in ((0, px), (1, py)):
                where = pl.ds(u * 32 + 2 * half + r, UNIT, stride=4)
                res = factor * plane - obs_ref[where, :]
                res_ref[where, :] = res
                total = total + res * res
        return total

    def leave(c):
        size = res_ref.shape[0] // chunks
        piece = pl.ds(pl.multiple_of(c * size, size), size)
        return pltpu.make_async_copy(res_ref.at[piece, :], res_hbm.at[piece, :], out_sems.at[c])

    def chunk(c, total):
        start(c + AHEAD)
        wait(c)

        def trip(i, total):
            first = (c * trips + i) * WAYS2
            for w in range(WAYS2):
                total = project(first + w, t1s[w], t2s[w], total)
            return total

        total = lax.fori_loop(0, trips, trip, total)
        leave(c).start()
        return total

    cost_ref[...] = lax.fori_loop(0, chunks, chunk, jnp.zeros((8, 128), jnp.float32))

    def left(c, carry):
        leave(c).wait()
        return carry

    lax.fori_loop(0, chunks, left, 0)


SMEM = pl.BlockSpec(memory_space=pltpu.SMEM)
VMEM = pl.BlockSpec(memory_space=pltpu.VMEM)
HBM = pl.BlockSpec(memory_space=pl.ANY)


def run_reduce(me, n_cam, tile_block, tile_points, table, cam_jac, point_jac, ids_cam, ids_pt, points):
    chunks = math.gcd(tile_block.shape[0] // (UNIT * WAYS), CHUNKS)
    streamed = (cam_jac, point_jac, ids_cam, ids_pt)
    return pl.pallas_call(
        functools.partial(reduce_kernel, n_cam),
        out_shape=(jax.ShapeDtypeStruct((3, points // 128 // n_cam, 128), jnp.float32),) * n_cam,
        in_specs=[SMEM] * 3 + [VMEM] + [HBM] * 4,
        out_specs=(VMEM,) * n_cam,
        scratch_shapes=[pltpu.VMEM(a.shape, a.dtype) for a in streamed]
        + [pltpu.SemaphoreType.DMA((chunks, len(streamed)))]
        + [pltpu.VMEM((GATHER * 24, 128), jnp.float32)]
        + [pltpu.VMEM((points // PB, 24, 128), jnp.float32)]
        + [pltpu.VMEM((2 * UNIT * PITCH, 128), jnp.float32)] * WAYS
        + [pltpu.VMEM((80, 128), jnp.float32)] * WAYS
        + [pltpu.VMEM((96, 128), jnp.float32)] * WAYS,
        name="reduce_points",
    )(me, tile_block, tile_points, table, *streamed)


def run_project(me, tile_block, tile_points, table, trial, obs_rows, ids_cam, ids_pt):
    chunks = math.gcd(tile_block.shape[0] // (UNIT * WAYS2), CHUNKS)
    streamed = (obs_rows, ids_cam, ids_pt)
    n_cam = len(trial)
    points = n_cam * trial[0].shape[1]
    return pl.pallas_call(
        functools.partial(project_kernel, n_cam),
        out_shape=(
            jax.ShapeDtypeStruct(obs_rows.shape, jnp.float32),
            jax.ShapeDtypeStruct((8, 128), jnp.float32),
        ),
        in_specs=[SMEM] * 3 + [VMEM] * (1 + n_cam) + [HBM] * 3,
        out_specs=(HBM, VMEM),
        scratch_shapes=[pltpu.VMEM(a.shape, a.dtype) for a in streamed]
        + [pltpu.VMEM(obs_rows.shape, jnp.float32)]
        + [pltpu.SemaphoreType.DMA((chunks, len(streamed))), pltpu.SemaphoreType.DMA((chunks,))]
        + [pltpu.VMEM((points * 4, 128), jnp.float32)]
        + [pltpu.VMEM((144, 128), jnp.float32)] * WAYS2
        + [pltpu.VMEM((72, 128), jnp.float32)] * WAYS2,
        name="project_points",
    )(me, tile_block, tile_points, table, *trial, *streamed)


def rotation_rows(cameras, increment):
    trial = cameras + increment
    w = trial[:, 0:3]
    size = jnp.sqrt(jnp.sum(w * w, axis=1))
    cosine = jnp.cos(size)
    s1 = jnp.sinc(size / math.pi)
    s2 = 0.5 * jnp.square(jnp.sinc(size / (2.0 * math.pi)))
    w = [w[:, 0], w[:, 1], w[:, 2]]
    rows = [
        cosine + s2 * w[0] * w[0],
        s2 * w[0] * w[1] - s1 * w[2],
        s2 * w[0] * w[2] + s1 * w[1],
        s2 * w[1] * w[0] + s1 * w[2],
        cosine + s2 * w[1] * w[1],
        s2 * w[1] * w[2] - s1 * w[0],
        s2 * w[2] * w[0] - s1 * w[1],
        s2 * w[2] * w[1] + s1 * w[0],
        cosine + s2 * w[2] * w[2],
    ]
    rows += [trial[:, m] for m in range(3, 9)] + [cosine]
    return jnp.stack(rows, axis=1)


def spread(value, axis, size):
    parts = [value]
    for s in range(1, size):
        parts.append(lax.ppermute(value, axis, [(k, (k + s) % size) for k in range(size)]))
    return parts


def on_device(
    n_pts,
    n_cam,
    cameras,
    increment,
    points,
    point_gradient,
    point_inverse,
    cam_jacobian,
    point_jacobian,
    observed,
    tile_block,
    tile_points,
    obs_camera,
    obs_point,
    accept,
):
    both = ("pts", "cam")
    mine = jnp.concatenate([increment, cameras], axis=0)
    table = lax.all_to_all(
        jnp.broadcast_to(mine[None], (n_pts * n_cam,) + mine.shape), both, 0, 0
    )
    blocks = table.shape[0] * table.shape[2] // CB
    table = table.reshape(table.shape[0], 18, -1, CB).transpose(0, 2, 1, 3).reshape(blocks, 18, CB)
    rot_table = rotation_rows(table[:, 9:18], table[:, 0:9])

    count = obs_camera.shape[0]
    point_count = points.shape[1]
    ids_cam = obs_camera.reshape(-1, 128)
    ids_pt = obs_point.reshape(-1, 128)
    me = lax.axis_index("cam")
    me_word = me.reshape(1).astype(jnp.int32)
    parts = run_reduce(
        me_word, n_cam, tile_block, tile_points, table, cam_jacobian, point_jacobian, ids_cam, ids_pt, point_count
    )

    summed = parts[0]
    for s in range(1, n_cam):
        summed = summed + lax.ppermute(
            parts[s], "cam", [(k, (k + s) % n_cam) for k in range(n_cam)]
        )
    rows = point_count // 128 // n_cam

    def own(array):
        part = lax.dynamic_slice_in_dim(array, me * (rows * 128), rows * 128, 1)
        return part.reshape(array.shape[0], rows, 128)

    residue = own(point_gradient) - summed
    inverse = own(point_inverse)
    point_step = jnp.stack(
        [
            inverse[3 * i] * residue[0]
            + inverse[3 * i + 1] * residue[1]
            + inverse[3 * i + 2] * residue[2]
            for i in range(3)
        ]
    )
    trial = spread(own(points) + point_step, "cam", n_cam)

    obs_rows = observed.reshape(2, -1, 128).transpose(1, 0, 2).reshape(-1, 128)
    residual, partial = run_project(
        me_word, tile_block, tile_points, rot_table, trial, obs_rows, ids_cam, ids_pt
    )
    residual = residual.reshape(-1, 2, 128).transpose(1, 0, 2).reshape(2, -1)

    partial = jnp.sum(partial, axis=0, keepdims=True)
    spread_sums = lax.all_to_all(
        jnp.broadcast_to(partial, (n_pts * n_cam, 128)), both, 0, 0
    )
    trial_cost = jnp.sum(spread_sums) / (2.0 * count * n_pts * n_cam)
    flag = jnp.remainder(accept, 2).astype(jnp.float32)
    trial = jnp.take(jnp.stack(trial), jnp.mod(me - jnp.arange(n_cam), n_cam), axis=0)
    trial_natural = trial.transpose(1, 0, 2, 3).reshape(3, point_count)
    accepted_points = jnp.where(flag > 0.0, trial_natural, points)
    return residual, trial_cost, accepted_points, cameras + flag * increment


def solution(mesh):
    in_specs = (
        P(None, ("pts", "cam")),
        P(None, ("pts", "cam")),
        P(None, "pts"),
        P(None, "pts"),
        P(None, "pts"),
        P(None, ("pts", "cam")),
        P(None, ("pts", "cam")),
        P(None, ("pts", "cam")),
        P(("pts", "cam")),
        P(("pts", "cam")),
        P(("pts", "cam")),
        P(("pts", "cam")),
        P(),
    )
    out_specs = (P(None, ("pts", "cam")), P(), P(None, "pts"), P(None, ("pts", "cam")))
    body = functools.partial(on_device, mesh.shape["pts"], mesh.shape["cam"])
    return jax.shard_map(body, mesh=mesh, in_specs=in_specs, out_specs=out_specs, check_vma=False)
```

time: 163 us -> 110 us (0.67)
  Pallas kernels: 80.2 us -> 30.8 us
  waiting for transfers between devices: 35.8 us -> 33.1 us
    pallas_call x2, Pallas kernels: 80.2 us -> 30.8 us  [the longest x1 18.3 us: run_reduce(): pl.pallas_call(functools.partial(reduce_kernel, n_cam), out_shape=(jax.Sh...]
    ppermute x3, waiting for transfers between devices: 12.8 us -> 14.9 us  [on_device(): lax.ppermute(parts[s], 'cam', [(k, (k + s) % n_cam) for k in range(n_cam)])]
    all_to_all x1, waiting for transfers between devices: 6.42 us -> 4.44 us  [on_device(): lax.all_to_all(jnp.broadcast_to(mine[None], (n_pts * n_cam,) + mine.shape...]
    all_to_all x1, waiting for transfers between devices: 5.46 us -> 3.54 us  [on_device(): lax.all_to_all(jnp.broadcast_to(partial, (n_pts * n_cam, 128)), both, 0, 0)]
  transfers between devices with their start and end apart: 8 -> 8, of which waited for: 6 -> 6; matrix products, arithmetic and copies ran while one was open for 5% -> 11% of each run, Pallas kernels for 0% -> 0%
where the time goes in v2:
time: 110 us
  waiting for transfers between devices  33.1 us (30%)
  Pallas kernels  30.8 us (28%)
  starting transfers between devices  24.8 us (23%)
  local copies, waits for them, and re-layouts  10.1 us (9%)
  other arithmetic  7.82 us (7%)
  between operations  3.29 us (3%)
    pallas_call x1, Pallas kernels, run_reduce(): pl.pallas_call(functools.partial(reduce_kernel, n_cam), out_shape=(jax.Sh...  18.3 us
    ppermute x3, waiting for transfers between devices, on_device(): lax.ppermute(parts[s], 'cam', [(k, (k + s) % n_cam) for k in range(n_cam)])  14.9 us
    pallas_call x1, Pallas kernels, run_project(): pl.pallas_call(functools.partial(project_kernel, n_cam), out_shape=(jax.S...  12.5 us
    ppermute x3, waiting for transfers between devices, spread(): lax.ppermute(value, axis, [(k, (k + s) % size) for k in range(size)])  10.2 us
    all_to_all x1, starting transfers between devices, on_device(): lax.all_to_all(jnp.broadcast_to(partial, (n_pts * n_cam, 128)), both, 0, 0)  8.1 us
    all_to_all x1, starting transfers between devices, on_device(): lax.all_to_all(jnp.broadcast_to(mine[None], (n_pts * n_cam,) + mine.shape...  7.33 us
    ppermute x3, starting transfers between devices, spread(): lax.ppermute(value, axis, [(k, (k + s) % size) for k in range(size)])  5.74 us
    all_to_all x1, waiting for transfers between devices, on_device(): lax.all_to_all(jnp.broadcast_to(mine[None], (n_pts * n_cam,) + mine.shape...  4.44 us
  transfers between devices with their start and end apart: 8, of which 6 were waited for; matrix products, arithmetic and copies ran while one was open for 11% of the time, Pallas kernels for 0%

profile of v2, /device:TPU:0, one launch (start us, length us, event | category | flops | bytes accessed | tf_op | source)
XLA Modules:
  0.0 109.9 jit_solution(2002571547630297527)
XLA Ops:
  0.6 0.0 copy-start
  0.6 0.8 pad_maximum_fusion.1
  1.5 0.8 broadcast_in_dim.25
  2.2 7.3 %all-to-all-start = ((f32[32,18,128]{2,1,0:T(8,128)}), f32[32,18,128]{2,1,0:T(8,128)S(1)}, u32[]{:S(2)}, u32[]{:S(2)}) async-start(f32[32,18,128]{2,1,0:T(8,128)} %broadcast_in_dim.25), calls=%async_computation | async-start | bytes 786432 | tf_op jit(solution)/shard_map/all_to_all | solution.py:392
  10.3 4.3 %constant_dynamic-slice_fusion = (f32[1,16384]{1,0:T(1,128)S(1)}, f32[1,16384]{1,0:T(1,128)S(1)}, f32[1,16384]{1,0:T(1,128)S(1)}, f32[1,16384]{1,0:T(1,128)S(1)}...) fusion(f32[9,65536]{1,0:T(8,128)} %param.18, ...), kind=kLoop, calls=%fused_computation.94 | loop fusion | bytes 1179684 | tf_op jit(solution)/shard_map/slice | solution.py:424
  14.6 0.0 copy-done
  14.6 0.1 dynamic-slice_bitcast_fusion
  14.6 1.0 dynamic-slice_bitcast_fusion.1
  15.6 1.3 %multiply_add_fusion.11 = f32[9,128]{1,0:T(8,128)} fusion(f32[9,128]{1,0:T(8,128)} %param.14, f32[9,128]{1,0:T(8,128)} %param.15, f32[]{:T(128)S(6)} %convert_element_type.6), kind=kLoop, calls=%fused_computation.83 | loop fusion | flops 2304 | bytes 13828 | tf_op jit(solution)/shard_map/add | solution.py:447
  17.0 4.4 %all-to-all-done.tab_ref = f32[32,18,128]{2,1,0:T(8,128)S(1)} async-done(((f32[32,18,128]{2,1,0:T(8,128)}), f32[32,18,128]{2,1,0:T(8,128)S(1)}, u32[]{:S(2)}, u32[]{:S(2)}) %all-to-all-start) | async-done | bytes 294944 | tf_op jit(solution)/shard_map/all_to_all | solution.py:392
  21.4 0.0 copy-start.1
  21.4 0.1 copy_add_fusion
  21.6 0.1 multiply_add_fusion.5
  21.7 0.1 multiply_add_fusion.6
  21.8 0.1 copy.85
  21.9 0.3 copy-done.1
  22.2 18.3 %reduce_points.1 = (f32[3,128,128]{2,1,0:T(8,128)}, f32[3,128,128]{2,1,0:T(8,128)}, f32[3,128,128]{2,1,0:T(8,128)}, f32[3,128,128]{2,1,0:T(8,128)}) custom-call(s32[1]{0:T(128)} %bitcast.me_ref, s32[1024]{0:T(1024)} %tb_ref.3, s32[1024]{0:T(1024)} %tp_ref.3, f32[32,18,128]{2,1,0:T(8,128)} %copy-done.1, bf16[18,262144]{1,0:T(8,128)(2,1)} %cj_hbm.1, ...), custom_call_target="tpu_custom_call" | custom-call | tf_op jit(solution)/shard_map/reduce_points/pallas_call | solution.py:304
  40.5 2.6 %collective-permute-start.2 = (f32[3,128,128]{2,1,0:T(8,128)}, f32[3,128,128]{2,1,0:T(8,128)S(1)}, u32[]{:S(2)}, u32[]{:S(2)}) collective-permute-start(f32[3,128,128]{2,1,0:T(8,128)} %get-tuple-element.14), channel_id=1, source_target_pairs={{0,3},{1,0},{2,1},{3,2},{4,7},{5,4},{6,5},{7,6},{8,11},{9,8},{10,9... | collective-permute-start | bytes 589832 | tf_op jit(solution)/shard_map/ppermute | solution.py:411
  43.1 1.1 collective-permute-start.1
  44.1 0.0 collective-permute-start
  44.1 1.6 %stack.67.tab_ref = f32[32,16,128]{2,1,0:T(8,128)} concatenate(f32[32,1,128]{2,1,0:T(1,128)S(1)} %bitcast.166, f32[32,1,128]{2,1,0:T(1,128)S(1)} %bitcast.171, f32[32,1,128]{2,1,0:T(1,128)S(1)} %bitcast.170, f32[32,1,128]{2,1,0:T(1,128)S(1)} %bitcast.169, f32[32,1,128]{2,1,0:T(1,128)S(1)} %bitcast.165, f32[32,1,128]{2,1,0:T(1,128)S(1)} %bitcast.172, f32[32,1,128]{2,1,0:T(1,128)S(1)} %bitcast.168, ...), dimensions={1} | concatenate | bytes 524288 | tf_op jit(solution)/shard_map/stack | solution.py:363
  45.7 4.4 %collective-permute-done.2 = f32[3,128,128]{2,1,0:T(8,128)S(1)} collective-permute-done((f32[3,128,128]{2,1,0:T(8,128)}, f32[3,128,128]{2,1,0:T(8,128)S(1)}, u32[]{:S(2)}, u32[]{:S(2)}) %collective-permute-start.2) | collective-permute-done | bytes 196640 | tf_op jit(solution)/shard_map/ppermute | solution.py:411
  50.1 10.6 %collective-permute-done.1 = f32[3,128,128]{2,1,0:T(8,128)S(1)} collective-permute-done((f32[3,128,128]{2,1,0:T(8,128)}, f32[3,128,128]{2,1,0:T(8,128)S(1)}, u32[]{:S(2)}, u32[]{:S(2)}) %collective-permute-start.1) | collective-permute-done | bytes 196640 | tf_op jit(solution)/shard_map/ppermute | solution.py:411
  60.6 0.0 collective-permute-done
  60.6 1.0 bitcast_subtract_fusion
  61.7 0.0 copy-start.5
  61.7 1.0 collective-permute-start.3
  62.7 1.9 %collective-permute-start.4 = (f32[3,128,128]{2,1,0:T(8,128)S(1)}, f32[3,128,128]{2,1,0:T(8,128)S(1)}, u32[]{:S(2)}, u32[]{:S(2)}) collective-permute-start(f32[3,128,128]{2,1,0:T(8,128)S(1)} %bitcast_add_fusion.1.refs_0_), channel_id=1, source_target_pairs={{0,2},{1,3},{2,0},{3,1},{4,6},{5,7},{6,4},{7,5},{8,10},{9,11},{10,... | collective-permute-start | bytes 589832 | tf_op jit(solution)/shard_map/ppermute | solution.py:369
  64.6 2.8 %collective-permute-start.5 = (f32[3,128,128]{2,1,0:T(8,128)S(1)}, f32[3,128,128]{2,1,0:T(8,128)S(1)}, u32[]{:S(2)}, u32[]{:S(2)}) collective-permute-start(f32[3,128,128]{2,1,0:T(8,128)S(1)} %bitcast_add_fusion.1.refs_0_), channel_id=1, source_target_pairs={{0,3},{1,0},{2,1},{3,2},{4,7},{5,4},{6,5},{7,6},{8,11},{9,8},{10,9... | collective-permute-start | bytes 589832 | tf_op jit(solution)/shard_map/ppermute | solution.py:369
  67.5 3.3 %collective-permute-done.3.refs_1_ = f32[3,128,128]{2,1,0:T(8,128)S(1)} collective-permute-done((f32[3,128,128]{2,1,0:T(8,128)S(1)}, f32[3,128,128]{2,1,0:T(8,128)S(1)}, u32[]{:S(2)}, u32[]{:S(2)}) %collective-permute-start.3) | collective-permute-done | bytes 196640 | tf_op jit(solution)/shard_map/ppermute | solution.py:369
  70.8 0.0 copy-start.2
  70.8 6.9 %collective-permute-done.4.refs_2_ = f32[3,128,128]{2,1,0:T(8,128)S(1)} collective-permute-done((f32[3,128,128]{2,1,0:T(8,128)S(1)}, f32[3,128,128]{2,1,0:T(8,128)S(1)}, u32[]{:S(2)}, u32[]{:S(2)}) %collective-permute-start.4) | collective-permute-done | bytes 196640 | tf_op jit(solution)/shard_map/ppermute | solution.py:369
  77.7 0.0 collective-permute-done.5.refs_3_
  77.7 0.0 copy-done.5
  77.7 0.0 copy-done.2
  77.7 0.7 copy-done.3
  78.4 0.1 copy-done.4
  78.5 12.5 %project_points.1 = (f32[4096,128]{1,0:T(8,128)}, f32[8,128]{1,0:T(8,128)}) custom-call(s32[1]{0:T(128)} %bitcast.me_ref, s32[1024]{0:T(1024)} %tb_ref.3, s32[1024]{0:T(1024)} %tp_ref.3, f32[32,16,128]{2,1,0:T(8,128)} %stack.67.tab_ref, f32[3,128,128]{2,1,0:T(8,128)} %copy-done.5, f32[3,128,128]{2,1,0:T(8,128)} %copy-done.2, f32[3,128,128]{2,1,0:T(8,128)} %copy-done.3, ...), custom_call_target="tpu_custom_call" | custom-call | tf_op jit(solution)/shard_map/project_points/pallas_call | solution.py:325
  91.0 0.7 reduce_sum.28
  91.6 0.6 broadcast_in_dim.26
  92.3 8.1 %all-to-all-start.1 = ((f32[32,1,128]{2,1,0:T(1,128)}), f32[32,1,128]{2,1,0:T(1,128)S(1)}, u32[]{:S(2)}, u32[]{:S(2)}) async-start(f32[32,1,128]{2,1,0:T(1,128)} %broadcast_in_dim.26), calls=%async_computation.1 | async-start | bytes 32768 | tf_op jit(solution)/shard_map/all_to_all | solution.py:439
  100.4 1.2 %pad_maximum_fusion = f32[4,3,128,128]{3,2,1,0:T(8,128)S(1)} fusion(f32[1,3,128,128]{3,2,1,0:T(8,128)} %bitcast.151, f32[1,3,128,128]{3,2,1,0:T(8,128)} %bitcast.150, f32[1,3,128,128]{3,2,1,0:T(8,128)} %bitcast.149, f32[1,3,128,128]{3,2,1,0:T(8,128)S(1)} %bitcast_add_fusion), kind=kLoop, calls=%fused_computation.2 | loop fusion | flops 589824 | bytes 1572864 | tf_op jit(solution)/shard_map/stack | solution.py:444
  101.5 0.6 gather_fusion
  102.1 0.1 select_bitcast_fusion
  102.3 0.1 copy.89
  102.3 1.7 %bitcast_select_fusion = f32[3,65536]{1,0:T(4,128)} fusion(f32[3,65536]{1,0:T(4,128)} %param.16, f32[1,3,512,128]{3,2,1,0:T(8,128)S(1)} %bitcast.147, pred[]{:T(512)S(6)} %gt.3), kind=kLoop, calls=%fused_computation.1 | loop fusion | flops 196608 | bytes 2359297 | tf_op jit(solution)/shard_map/jit(_where)/select_n | solution.py:446
  104.0 3.5 %all-to-all-done.1 = f32[32,1,128]{2,1,0:T(1,128)S(1)} async-done(((f32[32,1,128]{2,1,0:T(1,128)}), f32[32,1,128]{2,1,0:T(1,128)S(1)}, u32[]{:S(2)}, u32[]{:S(2)}) %all-to-all-start.1) | async-done | bytes 16416 | tf_op jit(solution)/shard_map/all_to_all | solution.py:439
  107.6 0.6 reduce_sum.29
  (12 shorter events, 0.2 us)
Async XLA Ops:
  0.6 13.9 %copy-start = (f32[3,65536]{1,0:T(4,128)S(1)}, f32[3,65536]{1,0:T(4,128)}, u32[]{:S(2)}) copy-start(f32[3,65536]{1,0:T(4,128)} %param.17) | copy-start | bytes 2359300
  2.2 19.2 %all-to-all-start = ((f32[32,18,128]{2,1,0:T(8,128)}), f32[32,18,128]{2,1,0:T(8,128)S(1)}, u32[]{:S(2)}, u32[]{:S(2)}) async-start(f32[32,18,128]{2,1,0:T(8,128)} %broadcast_in_dim.25), calls=%async_computation | async-start | bytes 786432 | tf_op jit(solution)/shard_map/all_to_all | solution.py:392
  21.4 0.7 copy-start.1
  40.5 9.6 %collective-permute-start.2 = (f32[3,128,128]{2,1,0:T(8,128)}, f32[3,128,128]{2,1,0:T(8,128)S(1)}, u32[]{:S(2)}, u32[]{:S(2)}) collective-permute-start(f32[3,128,128]{2,1,0:T(8,128)} %get-tuple-element.14), channel_id=1, source_target_pairs={{0,3},{1,0},{2,1},{3,2},{4,7},{5,4},{6,5},{7,6},{8,11},{9,8},{10,9... | collective-permute-start | bytes 589832 | tf_op jit(solution)/shard_map/ppermute | solution.py:411
  43.1 17.6 %collective-permute-start.1 = (f32[3,128,128]{2,1,0:T(8,128)}, f32[3,128,128]{2,1,0:T(8,128)S(1)}, u32[]{:S(2)}, u32[]{:S(2)}) collective-permute-start(f32[3,128,128]{2,1,0:T(8,128)} %get-tuple-element.13), channel_id=1, source_target_pairs={{0,2},{1,3},{2,0},{3,1},{4,6},{5,7},{6,4},{7,5},{8,10},{9,11},{10,... | collective-permute-start | bytes 589832 | tf_op jit(solution)/shard_map/ppermute | solution.py:411
  44.1 16.5 %collective-permute-start = (f32[3,128,128]{2,1,0:T(8,128)}, f32[3,128,128]{2,1,0:T(8,128)S(1)}, u32[]{:S(2)}, u32[]{:S(2)}) collective-permute-start(f32[3,128,128]{2,1,0:T(8,128)} %get-tuple-element.12), channel_id=1, source_target_pairs={{0,1},{1,2},{2,3},{3,0},{4,5},{5,6},{6,7},{7,4},{8,9},{9,10},{10,1... | collective-permute-start | bytes 589832 | tf_op jit(solution)/shard_map/ppermute | solution.py:411
  61.7 16.0 %copy-start.5 = (f32[3,128,128]{2,1,0:T(8,128)}, f32[3,128,128]{2,1,0:T(8,128)S(1)}, u32[]{:S(2)}) copy-start(f32[3,128,128]{2,1,0:T(8,128)S(1)} %bitcast_add_fusion.1.refs_0_) | copy-start | bytes 589828
  61.7 9.0 %collective-permute-start.3 = (f32[3,128,128]{2,1,0:T(8,128)S(1)}, f32[3,128,128]{2,1,0:T(8,128)S(1)}, u32[]{:S(2)}, u32[]{:S(2)}) collective-permute-start(f32[3,128,128]{2,1,0:T(8,128)S(1)} %bitcast_add_fusion.1.refs_0_), channel_id=1, source_target_pairs={{0,1},{1,2},{2,3},{3,0},{4,5},{5,6},{6,7},{7,4},{8,9},{9,10},{10,1... | collective-permute-start | bytes 589832 | tf_op jit(solution)/shard_map/ppermute | solution.py:369
  62.7 15.0 %collective-permute-start.4 = (f32[3,128,128]{2,1,0:T(8,128)S(1)}, f32[3,128,128]{2,1,0:T(8,128)S(1)}, u32[]{:S(2)}, u32[]{:S(2)}) collective-permute-start(f32[3,128,128]{2,1,0:T(8,128)S(1)} %bitcast_add_fusion.1.refs_0_), channel_id=1, source_target_pairs={{0,2},{1,3},{2,0},{3,1},{4,6},{5,7},{6,4},{7,5},{8,10},{9,11},{10,... | collective-permute-start | bytes 589832 | tf_op jit(solution)/shard_map/ppermute | solution.py:369
  64.6 13.1 %collective-permute-start.5 = (f32[3,128,128]{2,1,0:T(8,128)S(1)}, f32[3,128,128]{2,1,0:T(8,128)S(1)}, u32[]{:S(2)}, u32[]{:S(2)}) collective-permute-start(f32[3,128,128]{2,1,0:T(8,128)S(1)} %bitcast_add_fusion.1.refs_0_), channel_id=1, source_target_pairs={{0,3},{1,0},{2,1},{3,2},{4,7},{5,4},{6,5},{7,6},{8,11},{9,8},{10,9... | collective-permute-start | bytes 589832 | tf_op jit(solution)/shard_map/ppermute | solution.py:369
  70.8 7.0 %copy-start.2 = (f32[3,128,128]{2,1,0:T(8,128)}, f32[3,128,128]{2,1,0:T(8,128)S(1)}, u32[]{:S(2)}) copy-start(f32[3,128,128]{2,1,0:T(8,128)S(1)} %collective-permute-done.3.refs_1_) | copy-start | bytes 589828
  77.7 0.7 copy-start.3
  77.7 0.7 copy-start.4
  92.3 15.3 %all-to-all-start.1 = ((f32[32,1,128]{2,1,0:T(1,128)}), f32[32,1,128]{2,1,0:T(1,128)S(1)}, u32[]{:S(2)}, u32[]{:S(2)}) async-start(f32[32,1,128]{2,1,0:T(1,128)} %broadcast_in_dim.26), calls=%async_computation.1 | async-start | bytes 32768 | tf_op jit(solution)/shard_map/all_to_all | solution.py:439

commit v3 on v2

--- a/solution.py
+++ b/solution.py
@@ -12,11 +12,14 @@
 PB = 256
 TILE = 256
 UNIT = 8
+LOOKED = 10
 HI = 8
 LO = 32
 PITCH = 28
 WAYS = 16
 WAYS2 = 16
+WAYS3 = 8
+WORK = 1 << 24
 CHUNKS = 8
 GATHER = 16
 AHEAD = 2
@@ -135,8 +138,8 @@
                     )
                 )
             both = lax.dot_general(
-                jnp.concatenate(left, axis=1).astype(jnp.bfloat16),
-                jnp.concatenate(right, axis=1).astype(jnp.bfloat16),
+                jnp.concatenate(left, axis=1),
+                jnp.concatenate(right, axis=1),
                 (((1,), (1,)), ((), ())),
                 preferred_element_type=jnp.float32,
             )
@@ -197,21 +200,65 @@
         lax.fori_loop(0, groups // gather, part, 0)
 
 
-def project_kernel(
-    n_cam, me_ref, tb_ref, tp_ref, tab_ref, *refs
+def look_kernel(after_ref, tb_ref, tab_ref, cam_hbm, out_hbm, cam_ref, out_ref, sems, out_sems, *t1s):
+    chunks = sems.shape[0]
+    trips = cam_ref.shape[0] // (2 * UNIT * WAYS3 * chunks)
+    start, wait = arrivals(chunks, ((cam_hbm, cam_ref, 0),), sems)
+    for c in range(AHEAD):
+        start(c)
+
+    def look(u, t1):
+        for s in range(UNIT):
+            b = tb_ref[u * UNIT + s]
+            t1[pl.ds(s, 8, stride=9), :] = tab_ref[b, 0:8, :]
+            t1[pl.ds(72 + s, 8, stride=9), :] = tab_ref[b, 8:16, :]
+        for half in range(2):
+            ids = cam_ref[pl.ds(u * 16 + half, UNIT, stride=2), :]
+            base = (u * 2 + half) * (LOOKED * 8)
+            for m in range(LOOKED):
+                out_ref[pl.ds(pl.multiple_of(base + m * 8, 8), 8), :] = lanes(
+                    t1[m * 9 : m * 9 + 8, :], ids
+                )
+
+    def leave(c):
+        size = out_ref.shape[0] // chunks
+        piece = pl.ds(pl.multiple_of(c * size, size), size)
+        return pltpu.make_async_copy(out_ref.at[piece, :], out_hbm.at[piece, :], out_sems.at[c])
+
+    def chunk(c, carry):
+        start(c + AHEAD)
+        wait(c)
+
+        def trip(i, carry):
+            for w in range(WAYS3):
+                look((c * trips + i) * WAYS3 + w, t1s[w])
+            return carry
+
+        lax.fori_loop(0, trips, trip, 0)
+        leave(c).start()
+        return carry
+
+    lax.fori_loop(0, chunks, chunk, 0)
+
+    def left(c, carry):
+        leave(c).wait()
+        return carry
+
+    lax.fori_loop(0, chunks, left, 0)
+
+
+def project_kernel(n_cam, me_ref, tp_ref, *refs):
+    project_body(me_ref, tp_ref, refs[:n_cam], *refs[n_cam:])
+
+
+def project_body(
+    me_ref, tp_ref, pts_refs, val_hbm, obs_hbm, pt_hbm, res_hbm, cost_ref,
+    val_ref, obs_ref, pt_ref, res_ref, sems, out_sems, ptab, *t2s
 ):
-    project_body(me_ref, tb_ref, tp_ref, tab_ref, refs[:n_cam], *refs[n_cam:])
-
-
-def project_body(
-    me_ref, tb_ref, tp_ref, tab_ref, pts_refs, obs_hbm, cam_hbm, pt_hbm, res_hbm, cost_ref,
-    obs_ref, cam_ref, pt_ref, res_ref, sems, out_sems, ptab, *scratch
-):
-    t1s, t2s = scratch[:WAYS2], scratch[WAYS2:]
     chunks = sems.shape[0]
-    trips = cam_ref.shape[0] // (2 * UNIT * WAYS2 * chunks)
+    trips = pt_ref.shape[0] // (2 * UNIT * WAYS2 * chunks)
     start, wait = arrivals(
-        chunks, ((obs_hbm, obs_ref, 0), (cam_hbm, cam_ref, 0), (pt_hbm, pt_ref, 0)), sems
+        chunks, ((val_hbm, val_ref, 0), (obs_hbm, obs_ref, 0), (pt_hbm, pt_ref, 0)), sems
     )
     for c in range(AHEAD):
         start(c)
@@ -228,16 +275,11 @@
 
         lax.fori_loop(0, per, fill, 0)
 
-    def project(u, t1, t2, total):
-        first_tile = u * UNIT
+    def project(u, t2, total):
         for s in range(UNIT):
-            b = tb_ref[first_tile + s]
-            t1[pl.ds(s, 8, stride=9), :] = tab_ref[b, 0:8, :]
-            t1[pl.ds(72 + s, 8, stride=9), :] = tab_ref[b, 8:16, :]
-            p = tp_ref[first_tile + s]
+            p = tp_ref[u * UNIT + s]
             t2[pl.ds(s, 8, stride=9), :] = ptab[pl.ds(pl.multiple_of(p * 8, 8), 8), :]
         for half in range(2):
-            ids = cam_ref[pl.ds(u * 16 + half, UNIT, stride=2), :]
             pid = pt_ref[pl.ds(u * 16 + half, UNIT, stride=2), :]
             low = pid & 127
             upper = pid >= 128
@@ -249,15 +291,25 @@
                 )
                 for n in range(3)
             ]
-            q = [lanes(t1[m * 9 : m * 9 + 8, :], ids) for m in range(15)]
-            placed = [
-                q[3 * n] * x[0] + q[3 * n + 1] * x[1] + q[3 * n + 2] * x[2] + q[9 + n]
-                for n in range(3)
+            base = (u * 2 + half) * (LOOKED * 8)
+            q = [
+                val_ref[pl.ds(pl.multiple_of(base + m * 8, 8), 8), :] for m in range(LOOKED)
             ]
+
+            def cross(a, b):
+                return [
+                    a[1] * b[2] - a[2] * b[1],
+                    a[2] * b[0] - a[0] * b[2],
+                    a[0] * b[1] - a[1] * b[0],
+                ]
+
+            turned = cross(q[0:3], x)
+            again = cross(q[0:3], turned)
+            placed = [x[n] + q[3] * turned[n] + again[n] + q[4 + n] for n in range(3)]
             depth = jnp.maximum(-placed[2], 1.0)
             px, py = placed[0] / depth, placed[1] / depth
             radius = px * px + py * py
-            factor = q[12] * (1.0 + q[13] * radius + q[14] * radius * radius)
+            factor = q[7] * (1.0 + q[8] * radius + q[9] * radius * radius)
             for r, plane in ((0, px), (1, py)):
                 where = pl.ds(u * 32 + 2 * half + r, UNIT, stride=4)
                 res = factor * plane - obs_ref[where, :]
@@ -277,14 +329,16 @@
         def trip(i, total):
             first = (c * trips + i) * WAYS2
             for w in range(WAYS2):
-                total = project(first + w, t1s[w], t2s[w], total)
+                total = project(first + w, t2s[w], total)
             return total
 
         total = lax.fori_loop(0, trips, trip, total)
         leave(c).start()
         return total
 
-    cost_ref[...] = lax.fori_loop(0, chunks, chunk, jnp.zeros((8, 128), jnp.float32))
+    total = lax.fori_loop(0, chunks, chunk, jnp.zeros((8, 128), jnp.float32))
+    total = jnp.sum(total, axis=0, keepdims=True)
+    cost_ref[...] = jnp.broadcast_to(total[None], cost_ref.shape)
 
     def left(c, carry):
         leave(c).wait()
@@ -317,50 +371,56 @@
     )(me, tile_block, tile_points, table, *streamed)
 
 
-def run_project(me, tile_block, tile_points, table, trial, obs_rows, ids_cam, ids_pt):
-    chunks = math.gcd(tile_block.shape[0] // (UNIT * WAYS2), CHUNKS)
-    streamed = (obs_rows, ids_cam, ids_pt)
+def run_look(after, tile_block, table, ids_cam):
+    chunks = math.gcd(tile_block.shape[0] // (UNIT * WAYS3), CHUNKS)
+    rows = ids_cam.shape[0] * LOOKED
+    return pl.pallas_call(
+        look_kernel,
+        out_shape=jax.ShapeDtypeStruct((rows, 128), jnp.float32),
+        in_specs=[HBM, SMEM, VMEM, HBM],
+        out_specs=HBM,
+        scratch_shapes=[
+            pltpu.VMEM(ids_cam.shape, ids_cam.dtype),
+            pltpu.VMEM((rows, 128), jnp.float32),
+            pltpu.SemaphoreType.DMA((chunks, 1)),
+            pltpu.SemaphoreType.DMA((chunks,)),
+        ]
+        + [pltpu.VMEM((144, 128), jnp.float32)] * WAYS3,
+        cost_estimate=pl.CostEstimate(flops=WORK, bytes_accessed=rows * 512, transcendentals=0),
+        name="look_up_cameras",
+    )(after, tile_block, table, ids_cam)
+
+
+def run_project(me, senders, tile_points, trial, values, obs_rows, ids_pt):
+    chunks = math.gcd(tile_points.shape[0] // (UNIT * WAYS2), CHUNKS)
+    streamed = (values, obs_rows, ids_pt)
     n_cam = len(trial)
     points = n_cam * trial[0].shape[1]
     return pl.pallas_call(
         functools.partial(project_kernel, n_cam),
         out_shape=(
             jax.ShapeDtypeStruct(obs_rows.shape, jnp.float32),
-            jax.ShapeDtypeStruct((8, 128), jnp.float32),
+            jax.ShapeDtypeStruct((senders, 1, 128), jnp.float32),
         ),
-        in_specs=[SMEM] * 3 + [VMEM] * (1 + n_cam) + [HBM] * 3,
+        in_specs=[SMEM] * 2 + [VMEM] * n_cam + [HBM] * 3,
         out_specs=(HBM, VMEM),
         scratch_shapes=[pltpu.VMEM(a.shape, a.dtype) for a in streamed]
         + [pltpu.VMEM(obs_rows.shape, jnp.float32)]
         + [pltpu.SemaphoreType.DMA((chunks, len(streamed))), pltpu.SemaphoreType.DMA((chunks,))]
         + [pltpu.VMEM((points * 4, 128), jnp.float32)]
-        + [pltpu.VMEM((144, 128), jnp.float32)] * WAYS2
         + [pltpu.VMEM((72, 128), jnp.float32)] * WAYS2,
         name="project_points",
-    )(me, tile_block, tile_points, table, *trial, *streamed)
-
-
-def rotation_rows(cameras, increment):
+    )(me, tile_points, *trial, *streamed)
+
+
+def trial_rows(cameras, increment):
     trial = cameras + increment
     w = trial[:, 0:3]
-    size = jnp.sqrt(jnp.sum(w * w, axis=1))
-    cosine = jnp.cos(size)
-    s1 = jnp.sinc(size / math.pi)
-    s2 = 0.5 * jnp.square(jnp.sinc(size / (2.0 * math.pi)))
-    w = [w[:, 0], w[:, 1], w[:, 2]]
-    rows = [
-        cosine + s2 * w[0] * w[0],
-        s2 * w[0] * w[1] - s1 * w[2],
-        s2 * w[0] * w[2] + s1 * w[1],
-        s2 * w[1] * w[0] + s1 * w[2],
-        cosine + s2 * w[1] * w[1],
-        s2 * w[1] * w[2] - s1 * w[0],
-        s2 * w[2] * w[0] - s1 * w[1],
-        s2 * w[2] * w[1] + s1 * w[0],
-        cosine + s2 * w[2] * w[2],
-    ]
-    rows += [trial[:, m] for m in range(3, 9)] + [cosine]
-    return jnp.stack(rows, axis=1)
+    size = jnp.sqrt(jnp.sum(w * w, axis=1, keepdims=True))
+    vector = (math.sqrt(0.5) * jnp.sinc(size / (2.0 * math.pi))) * w
+    scalar = math.sqrt(2.0) * jnp.cos(0.5 * size)
+    rows = jnp.concatenate([vector, scalar, trial[:, 3:9]], axis=1)
+    return jnp.pad(rows, ((0, 0), (0, 16 - LOOKED), (0, 0)))
 
 
 def spread(value, axis, size):
@@ -394,7 +454,7 @@
     )
     blocks = table.shape[0] * table.shape[2] // CB
     table = table.reshape(table.shape[0], 18, -1, CB).transpose(0, 2, 1, 3).reshape(blocks, 18, CB)
-    rot_table = rotation_rows(table[:, 9:18], table[:, 0:9])
+    looked_table = trial_rows(table[:, 9:18], table[:, 0:9])
 
     count = obs_camera.shape[0]
     point_count = points.shape[1]
@@ -411,6 +471,7 @@
         summed = summed + lax.ppermute(
             parts[s], "cam", [(k, (k + s) % n_cam) for k in range(n_cam)]
         )
+    values = run_look(parts[0], tile_block, looked_table, ids_cam)
     rows = point_count // 128 // n_cam
 
     def own(array):
@@ -431,14 +492,11 @@
 
     obs_rows = observed.reshape(2, -1, 128).transpose(1, 0, 2).reshape(-1, 128)
     residual, partial = run_project(
-        me_word, tile_block, tile_points, rot_table, trial, obs_rows, ids_cam, ids_pt
+        me_word, n_pts * n_cam, tile_points, trial, values, obs_rows, ids_pt
     )
     residual = residual.reshape(-1, 2, 128).transpose(1, 0, 2).reshape(2, -1)
 
-    partial = jnp.sum(partial, axis=0, keepdims=True)
-    spread_sums = lax.all_to_all(
-        jnp.broadcast_to(partial, (n_pts * n_cam, 128)), both, 0, 0
-    )
+    spread_sums = lax.all_to_all(partial, both, 0, 0)
     trial_cost = jnp.sum(spread_sums) / (2.0 * count * n_pts * n_cam)
     flag = jnp.remainder(accept, 2).astype(jnp.float32)
     trial = jnp.take(jnp.stack(trial), jnp.mod(me - jnp.arange(n_cam), n_cam), axis=0)

time: 110 us -> 104 us (0.945)
  waiting for transfers between devices: 33.1 us -> 24.5 us
  Pallas kernels: 30.8 us -> 34.1 us
  local copies, waits for them, and re-layouts: 10.1 us -> 8.27 us
    ppermute x3, waiting for transfers between devices: 14.9 us -> 6.42 us  [on_device(): lax.ppermute(parts[s], 'cam', [(k, (k + s) % n_cam) for k in range(n_cam)])]
    pallas_call x0 -> x1, Pallas kernels: none -> 8.03 us  [run_look(): pl.pallas_call(look_kernel, out_shape=jax.ShapeDtypeStruct((rows, 128), j...]
    pallas_call x1, Pallas kernels: 12.5 us -> 9.45 us  [run_project(): pl.pallas_call(functools.partial(project_kernel, n_cam), out_shape=(jax.S...]
    pallas_call x1, Pallas kernels: 18.3 us -> 16.6 us  [run_reduce(): pl.pallas_call(functools.partial(reduce_kernel, n_cam), out_shape=(jax.Sh...]
    another operation x1 -> x0, local copies, waits for them, and re-layouts: 1.55 us -> none  [rotation_rows(): return jnp.stack(rows, axis=1)]
    unnamed x14 -> x16, local copies, waits for them, and re-layouts: 2.1 us -> 2.56 us
  transfers between devices with their start and end apart: 8 -> 8, of which waited for: 6 -> 5; matrix products, arithmetic and copies ran while one was open for 11% -> 12% of each run, Pallas kernels for 0% -> 8%
where the time goes in v3:
time: 104 us; the launch traced here: 103 us
  Pallas kernels  34.1 us (33%)
  starting transfers between devices  24.9 us (24%)
  waiting for transfers between devices  24.5 us (24%)
  local copies, waits for them, and re-layouts  8.27 us (8%)
  other arithmetic  7.94 us (8%)
  between operations  3.29 us (3%)
    pallas_call x1, Pallas kernels, run_reduce(): pl.pallas_call(functools.partial(reduce_kernel, n_cam), out_shape=(jax.Sh...  16.6 us
    ppermute x3, waiting for transfers between devices, spread(): lax.ppermute(value, axis, [(k, (k + s) % size) for k in range(size)])  10.2 us
    pallas_call x1, Pallas kernels, run_project(): pl.pallas_call(functools.partial(project_kernel, n_cam), out_shape=(jax.S...  9.45 us
    all_to_all x1, starting transfers between devices, on_device(): spread_sums = lax.all_to_all(partial, both, 0, 0)  8.17 us
    pallas_call x1, Pallas kernels, run_look(): pl.pallas_call(look_kernel, out_shape=jax.ShapeDtypeStruct((rows, 128), j...  8.03 us
    all_to_all x1, starting transfers between devices, on_device(): lax.all_to_all(jnp.broadcast_to(mine[None], (n_pts * n_cam,) + mine.shape...  7.33 us
    ppermute x3, waiting for transfers between devices, on_device(): lax.ppermute(parts[s], 'cam', [(k, (k + s) % n_cam) for k in range(n_cam)])  6.42 us
    ppermute x3, starting transfers between devices, spread(): lax.ppermute(value, axis, [(k, (k + s) % size) for k in range(size)])  5.76 us
  transfers between devices with their start and end apart: 8, of which 5 were waited for; matrix products, arithmetic and copies ran while one was open for 12% of the time, Pallas kernels for 8%

profile of v3, /device:TPU:0, one launch (start us, length us, event | category | flops | bytes accessed | tf_op | source)
XLA Modules:
  0.0 103.0 jit_solution(4888605803298165628)
XLA Ops:
  0.6 0.0 copy-start
  0.6 0.8 pad_maximum_fusion.1
  1.5 0.8 broadcast_in_dim.22
  2.2 7.3 %all-to-all-start = ((f32[32,18,128]{2,1,0:T(8,128)}), f32[32,18,128]{2,1,0:T(8,128)S(1)}, u32[]{:S(2)}, u32[]{:S(2)}) async-start(f32[32,18,128]{2,1,0:T(8,128)} %broadcast_in_dim.22), calls=%async_computation | async-start | bytes 786432 | tf_op jit(solution)/shard_map/all_to_all | solution.py:452
  10.3 4.3 %constant_dynamic-slice_fusion = (f32[1,16384]{1,0:T(1,128)S(1)}, f32[1,16384]{1,0:T(1,128)S(1)}, f32[1,16384]{1,0:T(1,128)S(1)}, f32[1,16384]{1,0:T(1,128)S(1)}...) fusion(f32[9,65536]{1,0:T(8,128)} %param.17, ...), kind=kLoop, calls=%fused_computation.55 | loop fusion | bytes 1179684 | tf_op jit(solution)/shard_map/slice | solution.py:485
  14.6 0.0 copy-done
  14.6 0.1 dynamic-slice_bitcast_fusion
  14.6 1.0 dynamic-slice_bitcast_fusion.1
  15.6 1.3 %multiply_add_fusion.4 = f32[9,128]{1,0:T(8,128)} fusion(f32[9,128]{1,0:T(8,128)} %param.13, f32[9,128]{1,0:T(8,128)} %param.14, f32[]{:T(128)S(6)} %convert_element_type.10), kind=kLoop, calls=%fused_computation.44 | loop fusion | flops 2304 | bytes 13828 | tf_op jit(solution)/shard_map/add | solution.py:505
  17.0 4.4 %all-to-all-done.tab_ref = f32[32,18,128]{2,1,0:T(8,128)S(1)} async-done(((f32[32,18,128]{2,1,0:T(8,128)}), f32[32,18,128]{2,1,0:T(8,128)S(1)}, u32[]{:S(2)}, u32[]{:S(2)}) %all-to-all-start) | async-done | bytes 294944 | tf_op jit(solution)/shard_map/all_to_all | solution.py:452
  21.4 0.0 copy-start.1
  21.4 0.7 copy-done.1
  22.2 16.6 %reduce_points.1 = (f32[3,128,128]{2,1,0:T(8,128)}, f32[3,128,128]{2,1,0:T(8,128)}, f32[3,128,128]{2,1,0:T(8,128)}, f32[3,128,128]{2,1,0:T(8,128)}) custom-call(s32[1]{0:T(128)} %bitcast.me_ref, s32[1024]{0:T(1024)} %tb_ref.3, s32[1024]{0:T(1024)} %tp_ref.3, f32[32,18,128]{2,1,0:T(8,128)} %copy-done.1, bf16[18,262144]{1,0:T(8,128)(2,1)} %cj_hbm.1, ...), custom_call_target="tpu_custom_call" | custom-call | tf_op jit(solution)/shard_map/reduce_points/pallas_call | solution.py:358
  38.8 2.6 %collective-permute-start.2 = (f32[3,128,128]{2,1,0:T(8,128)}, f32[3,128,128]{2,1,0:T(8,128)S(1)}, u32[]{:S(2)}, u32[]{:S(2)}) collective-permute-start(f32[3,128,128]{2,1,0:T(8,128)} %get-tuple-element.13), channel_id=1, source_target_pairs={{0,3},{1,0},{2,1},{3,2},{4,7},{5,4},{6,5},{7,6},{8,11},{9,8},{10,9... | collective-permute-start | bytes 589832 | tf_op jit(solution)/shard_map/ppermute | solution.py:471
  41.4 1.0 %collective-permute-start.1 = (f32[3,128,128]{2,1,0:T(8,128)}, f32[3,128,128]{2,1,0:T(8,128)S(1)}, u32[]{:S(2)}, u32[]{:S(2)}) collective-permute-start(f32[3,128,128]{2,1,0:T(8,128)} %get-tuple-element.12), channel_id=1, source_target_pairs={{0,2},{1,3},{2,0},{3,1},{4,6},{5,7},{6,4},{7,5},{8,10},{9,11},{10,... | collective-permute-start | bytes 589832 | tf_op jit(solution)/shard_map/ppermute | solution.py:471
  42.4 0.0 collective-permute-start
  42.4 1.1 %slice_add_fusion = f32[32,9,128]{2,1,0:T(8,128)S(1)} fusion(f32[32,18,128]{2,1,0:T(8,128)} %copy-done.1), kind=kLoop, calls=%fused_computation.7 | loop fusion | flops 36864 | bytes 442368 | tf_op jit(solution)/shard_map/add | solution.py:417
  43.5 0.1 fusion.12
  43.7 0.8 select_maximum_fusion.tab_ref
  44.5 0.0 copy-start.6
  44.5 8.0 %look_up_cameras.1.refs_4_ = f32[20480,128]{1,0:T(8,128)} custom-call(f32[3,128,128]{2,1,0:T(8,128)} %get-tuple-element.10.after_ref, s32[1024]{0:T(1024)} %tb_ref.3, f32[32,16,128]{2,1,0:T(8,128)} %select_maximum_fusion.tab_ref, s32[2048,128]{1,0:T(8,128)} %bitcast.52), custom_call_target="tpu_custom_call" | custom-call | flops 16777216 | bytes 10485760 | tf_op jit(solution)/shard_map/look_up_cameras/pallas_call | solution.py:377
  52.5 0.0 collective-permute-done.2
  52.5 6.4 %collective-permute-done.1 = f32[3,128,128]{2,1,0:T(8,128)S(1)} collective-permute-done((f32[3,128,128]{2,1,0:T(8,128)}, f32[3,128,128]{2,1,0:T(8,128)S(1)}, u32[]{:S(2)}, u32[]{:S(2)}) %collective-permute-start.1) | collective-permute-done | bytes 196640 | tf_op jit(solution)/shard_map/ppermute | solution.py:471
  58.9 0.0 collective-permute-done
  58.9 0.0 copy-done.6
  58.9 0.1 bitcast_subtract_fusion
  59.1 0.0 copy-start.5
  59.1 1.0 collective-permute-start.3
  60.1 1.9 %collective-permute-start.4 = (f32[3,128,128]{2,1,0:T(8,128)S(1)}, f32[3,128,128]{2,1,0:T(8,128)S(1)}, u32[]{:S(2)}, u32[]{:S(2)}) collective-permute-start(f32[3,128,128]{2,1,0:T(8,128)S(1)} %bitcast_add_fusion.1.refs_0_), channel_id=1, source_target_pairs={{0,2},{1,3},{2,0},{3,1},{4,6},{5,7},{6,4},{7,5},{8,10},{9,11},{10,... | collective-permute-start | bytes 589832 | tf_op jit(solution)/shard_map/ppermute | solution.py:429
  62.0 2.8 %collective-permute-start.5 = (f32[3,128,128]{2,1,0:T(8,128)S(1)}, f32[3,128,128]{2,1,0:T(8,128)S(1)}, u32[]{:S(2)}, u32[]{:S(2)}) collective-permute-start(f32[3,128,128]{2,1,0:T(8,128)S(1)} %bitcast_add_fusion.1.refs_0_), channel_id=1, source_target_pairs={{0,3},{1,0},{2,1},{3,2},{4,7},{5,4},{6,5},{7,6},{8,11},{9,8},{10,9... | collective-permute-start | bytes 589832 | tf_op jit(solution)/shard_map/ppermute | solution.py:429
  64.9 3.1 %collective-permute-done.3.refs_1_ = f32[3,128,128]{2,1,0:T(8,128)S(1)} collective-permute-done((f32[3,128,128]{2,1,0:T(8,128)S(1)}, f32[3,128,128]{2,1,0:T(8,128)S(1)}, u32[]{:S(2)}, u32[]{:S(2)}) %collective-permute-start.3) | collective-permute-done | bytes 196640 | tf_op jit(solution)/shard_map/ppermute | solution.py:429
  68.0 0.0 copy-start.2
  68.0 7.0 %collective-permute-done.4.refs_2_ = f32[3,128,128]{2,1,0:T(8,128)S(1)} collective-permute-done((f32[3,128,128]{2,1,0:T(8,128)S(1)}, f32[3,128,128]{2,1,0:T(8,128)S(1)}, u32[]{:S(2)}, u32[]{:S(2)}) %collective-permute-start.4) | collective-permute-done | bytes 196640 | tf_op jit(solution)/shard_map/ppermute | solution.py:429
  75.0 0.0 copy-start.3
  75.0 0.0 collective-permute-done.5.refs_3_
  75.0 0.0 copy-done.5
  75.0 0.0 copy-done.2
  75.0 0.7 copy-done.3
  75.7 0.1 copy-done.4
  75.8 9.4 %project_points.1 = (f32[4096,128]{1,0:T(8,128)}, f32[32,1,128]{2,1,0:T(1,128)}) custom-call(s32[1]{0:T(128)} %bitcast.me_ref, s32[1024]{0:T(1024)} %tp_ref.3, f32[3,128,128]{2,1,0:T(8,128)} %copy-done.5, f32[3,128,128]{2,1,0:T(8,128)} %copy-done.2, f32[3,128,128]{2,1,0:T(8,128)} %copy-done.3, f32[3,128,128]{2,1,0:T(8,128)} %copy-done.4, ...), custom_call_target="tpu_custom_call" | custom-call | tf_op jit(solution)/shard_map/project_points/pallas_call | solution.py:399
  85.2 8.2 %all-to-all-start.1 = ((f32[32,1,128]{2,1,0:T(1,128)}), f32[32,1,128]{2,1,0:T(1,128)S(1)}, u32[]{:S(2)}, u32[]{:S(2)}) async-start(f32[32,1,128]{2,1,0:T(1,128)} %get-tuple-element.15), calls=%async_computation.1 | async-start | bytes 32768 | tf_op jit(solution)/shard_map/all_to_all | solution.py:499
  93.4 1.2 %pad_maximum_fusion = f32[4,3,128,128]{3,2,1,0:T(8,128)S(1)} fusion(f32[1,3,128,128]{3,2,1,0:T(8,128)} %bitcast.57, f32[1,3,128,128]{3,2,1,0:T(8,128)} %bitcast.56, f32[1,3,128,128]{3,2,1,0:T(8,128)} %bitcast.55, f32[1,3,128,128]{3,2,1,0:T(8,128)S(1)} %bitcast_add_fusion), kind=kLoop, calls=%fused_computation.2 | loop fusion | flops 589824 | bytes 1572864 | tf_op jit(solution)/shard_map/stack | solution.py:502
  94.6 0.6 gather_fusion
  95.2 0.1 select_bitcast_fusion
  95.3 0.1 copy.21
  95.4 1.7 %bitcast_select_fusion = f32[3,65536]{1,0:T(4,128)} fusion(f32[3,65536]{1,0:T(4,128)} %param.15, f32[1,3,512,128]{3,2,1,0:T(8,128)S(1)} %bitcast.53, pred[]{:T(512)S(6)} %gt.3), kind=kLoop, calls=%fused_computation.1 | loop fusion | flops 196608 | bytes 2359297 | tf_op jit(solution)/shard_map/jit(_where)/select_n | solution.py:504
  97.1 3.5 %all-to-all-done.1 = f32[32,1,128]{2,1,0:T(1,128)S(1)} async-done(((f32[32,1,128]{2,1,0:T(1,128)}), f32[32,1,128]{2,1,0:T(1,128)S(1)}, u32[]{:S(2)}, u32[]{:S(2)}) %all-to-all-start.1) | async-done | bytes 16416 | tf_op jit(solution)/shard_map/all_to_all | solution.py:499
  100.6 0.6 reduce_sum.19
  (10 shorter events, 0.2 us)
Async XLA Ops:
  0.6 13.9 %copy-start = (f32[3,65536]{1,0:T(4,128)S(1)}, f32[3,65536]{1,0:T(4,128)}, u32[]{:S(2)}) copy-start(f32[3,65536]{1,0:T(4,128)} %param.16) | copy-start | bytes 2359300
  2.2 19.2 %all-to-all-start = ((f32[32,18,128]{2,1,0:T(8,128)}), f32[32,18,128]{2,1,0:T(8,128)S(1)}, u32[]{:S(2)}, u32[]{:S(2)}) async-start(f32[32,18,128]{2,1,0:T(8,128)} %broadcast_in_dim.22), calls=%async_computation | async-start | bytes 786432 | tf_op jit(solution)/shard_map/all_to_all | solution.py:452
  21.4 0.7 copy-start.1
  38.8 13.7 %collective-permute-start.2 = (f32[3,128,128]{2,1,0:T(8,128)}, f32[3,128,128]{2,1,0:T(8,128)S(1)}, u32[]{:S(2)}, u32[]{:S(2)}) collective-permute-start(f32[3,128,128]{2,1,0:T(8,128)} %get-tuple-element.13), channel_id=1, source_target_pairs={{0,3},{1,0},{2,1},{3,2},{4,7},{5,4},{6,5},{7,6},{8,11},{9,8},{10,9... | collective-permute-start | bytes 589832 | tf_op jit(solution)/shard_map/ppermute | solution.py:471
  41.4 17.6 %collective-permute-start.1 = (f32[3,128,128]{2,1,0:T(8,128)}, f32[3,128,128]{2,1,0:T(8,128)S(1)}, u32[]{:S(2)}, u32[]{:S(2)}) collective-permute-start(f32[3,128,128]{2,1,0:T(8,128)} %get-tuple-element.12), channel_id=1, source_target_pairs={{0,2},{1,3},{2,0},{3,1},{4,6},{5,7},{6,4},{7,5},{8,10},{9,11},{10,... | collective-permute-start | bytes 589832 | tf_op jit(solution)/shard_map/ppermute | solution.py:471
  42.4 16.5 %collective-permute-start = (f32[3,128,128]{2,1,0:T(8,128)}, f32[3,128,128]{2,1,0:T(8,128)S(1)}, u32[]{:S(2)}, u32[]{:S(2)}) collective-permute-start(f32[3,128,128]{2,1,0:T(8,128)} %get-tuple-element.11), channel_id=1, source_target_pairs={{0,1},{1,2},{2,3},{3,0},{4,5},{5,6},{6,7},{7,4},{8,9},{9,10},{10,1... | collective-permute-start | bytes 589832 | tf_op jit(solution)/shard_map/ppermute | solution.py:471
  44.5 14.5 %copy-start.6 = (f32[3,128,128]{2,1,0:T(8,128)S(1)}, f32[3,128,128]{2,1,0:T(8,128)}, u32[]{:S(2)}) copy-start(f32[3,128,128]{2,1,0:T(8,128)} %get-tuple-element.10.after_ref) | copy-start | bytes 589828
  59.1 16.0 %copy-start.5 = (f32[3,128,128]{2,1,0:T(8,128)}, f32[3,128,128]{2,1,0:T(8,128)S(1)}, u32[]{:S(2)}) copy-start(f32[3,128,128]{2,1,0:T(8,128)S(1)} %bitcast_add_fusion.1.refs_0_) | copy-start | bytes 589828
  59.1 8.9 %collective-permute-start.3 = (f32[3,128,128]{2,1,0:T(8,128)S(1)}, f32[3,128,128]{2,1,0:T(8,128)S(1)}, u32[]{:S(2)}, u32[]{:S(2)}) collective-permute-start(f32[3,128,128]{2,1,0:T(8,128)S(1)} %bitcast_add_fusion.1.refs_0_), channel_id=1, source_target_pairs={{0,1},{1,2},{2,3},{3,0},{4,5},{5,6},{6,7},{7,4},{8,9},{9,10},{10,1... | collective-permute-start | bytes 589832 | tf_op jit(solution)/shard_map/ppermute | solution.py:429
  60.1 14.9 %collective-permute-start.4 = (f32[3,128,128]{2,1,0:T(8,128)S(1)}, f32[3,128,128]{2,1,0:T(8,128)S(1)}, u32[]{:S(2)}, u32[]{:S(2)}) collective-permute-start(f32[3,128,128]{2,1,0:T(8,128)S(1)} %bitcast_add_fusion.1.refs_0_), channel_id=1, source_target_pairs={{0,2},{1,3},{2,0},{3,1},{4,6},{5,7},{6,4},{7,5},{8,10},{9,11},{10,... | collective-permute-start | bytes 589832 | tf_op jit(solution)/shard_map/ppermute | solution.py:429
  62.0 13.0 %collective-permute-start.5 = (f32[3,128,128]{2,1,0:T(8,128)S(1)}, f32[3,128,128]{2,1,0:T(8,128)S(1)}, u32[]{:S(2)}, u32[]{:S(2)}) collective-permute-start(f32[3,128,128]{2,1,0:T(8,128)S(1)} %bitcast_add_fusion.1.refs_0_), channel_id=1, source_target_pairs={{0,3},{1,0},{2,1},{3,2},{4,7},{5,4},{6,5},{7,6},{8,11},{9,8},{10,9... | collective-permute-start | bytes 589832 | tf_op jit(solution)/shard_map/ppermute | solution.py:429
  68.0 7.0 %copy-start.2 = (f32[3,128,128]{2,1,0:T(8,128)}, f32[3,128,128]{2,1,0:T(8,128)S(1)}, u32[]{:S(2)}) copy-start(f32[3,128,128]{2,1,0:T(8,128)S(1)} %collective-permute-done.3.refs_1_) | copy-start | bytes 589828
  75.0 0.7 copy-start.3
  75.0 0.7 copy-start.4
  85.2 15.4 %all-to-all-start.1 = ((f32[32,1,128]{2,1,0:T(1,128)}), f32[32,1,128]{2,1,0:T(1,128)S(1)}, u32[]{:S(2)}, u32[]{:S(2)}) async-start(f32[32,1,128]{2,1,0:T(1,128)} %get-tuple-element.15), calls=%async_computation.1 | async-start | bytes 32768 | tf_op jit(solution)/shard_map/all_to_all | solution.py:499

commit v4 on v3

--- a/solution.py
+++ b/solution.py
@@ -53,28 +53,24 @@
 
 
 def reduce_kernel(
-    n_cam, me_ref, tb_ref, tp_ref, tab_ref, cj_hbm, pj_hbm, cam_hbm, pt_hbm, *refs
+    n_cam, me_ref, tb_ref, tp_ref, tab_ref, cj_hbm, pj_hbm, cam_ref, pt_ref, *refs
 ):
     out_refs, refs = refs[:n_cam], refs[n_cam:]
     reduce_body(
-        me_ref, tb_ref, tp_ref, tab_ref, cj_hbm, pj_hbm, cam_hbm, pt_hbm, out_refs, *refs
+        me_ref, tb_ref, tp_ref, tab_ref, cj_hbm, pj_hbm, cam_ref, pt_ref, out_refs, *refs
     )
 
 
 def reduce_body(
-    me_ref, tb_ref, tp_ref, tab_ref, cj_hbm, pj_hbm, cam_hbm, pt_hbm, out_refs,
-    cj_ref, pj_ref, cam_ref, pt_ref, sems, fin, acc, *scratch
+    me_ref, tb_ref, tp_ref, tab_ref, cj_hbm, pj_hbm, cam_ref, pt_ref, out_refs,
+    cj_ref, pj_ref, sems, fin, acc, *scratch
 ):
     s1s = scratch[:WAYS]
     t1s = scratch[WAYS : 2 * WAYS]
     v1s = scratch[2 * WAYS : 3 * WAYS]
     chunks = sems.shape[0]
     trips = cam_ref.shape[0] // (2 * UNIT * WAYS * chunks)
-    start, wait = arrivals(
-        chunks,
-        ((cj_hbm, cj_ref, 1), (pj_hbm, pj_ref, 1), (cam_hbm, cam_ref, 0), (pt_hbm, pt_ref, 0)),
-        sems,
-    )
+    start, wait = arrivals(chunks, ((cj_hbm, cj_ref, 1), (pj_hbm, pj_ref, 1)), sems)
     for c in range(AHEAD):
         start(c)
     acc[...] = jnp.zeros_like(acc)
@@ -200,13 +196,7 @@
         lax.fori_loop(0, groups // gather, part, 0)
 
 
-def look_kernel(after_ref, tb_ref, tab_ref, cam_hbm, out_hbm, cam_ref, out_ref, sems, out_sems, *t1s):
-    chunks = sems.shape[0]
-    trips = cam_ref.shape[0] // (2 * UNIT * WAYS3 * chunks)
-    start, wait = arrivals(chunks, ((cam_hbm, cam_ref, 0),), sems)
-    for c in range(AHEAD):
-        start(c)
-
+def look_kernel(after_ref, tb_ref, tab_ref, cam_ref, out_ref, *t1s):
     def look(u, t1):
         for s in range(UNIT):
             b = tb_ref[u * UNIT + s]
@@ -220,31 +210,12 @@
                     t1[m * 9 : m * 9 + 8, :], ids
                 )
 
-    def leave(c):
-        size = out_ref.shape[0] // chunks
-        piece = pl.ds(pl.multiple_of(c * size, size), size)
-        return pltpu.make_async_copy(out_ref.at[piece, :], out_hbm.at[piece, :], out_sems.at[c])
-
-    def chunk(c, carry):
-        start(c + AHEAD)
-        wait(c)
-
-        def trip(i, carry):
-            for w in range(WAYS3):
-                look((c * trips + i) * WAYS3 + w, t1s[w])
-            return carry
-
-        lax.fori_loop(0, trips, trip, 0)
-        leave(c).start()
+    def trip(i, carry):
+        for w in range(WAYS3):
+            look(i * WAYS3 + w, t1s[w])
         return carry
 
-    lax.fori_loop(0, chunks, chunk, 0)
-
-    def left(c, carry):
-        leave(c).wait()
-        return carry
-
-    lax.fori_loop(0, chunks, left, 0)
+    lax.fori_loop(0, cam_ref.shape[0] // (2 * UNIT * WAYS3), trip, 0)
 
 
 def project_kernel(n_cam, me_ref, tp_ref, *refs):
@@ -252,16 +223,11 @@
 
 
 def project_body(
-    me_ref, tp_ref, pts_refs, val_hbm, obs_hbm, pt_hbm, res_hbm, cost_ref,
-    val_ref, obs_ref, pt_ref, res_ref, sems, out_sems, ptab, *t2s
+    me_ref, tp_ref, pts_refs, val_ref, obs_ref, pt_ref, res_hbm, cost_ref,
+    res_ref, out_sems, ptab, *t2s
 ):
-    chunks = sems.shape[0]
+    chunks = out_sems.shape[0]
     trips = pt_ref.shape[0] // (2 * UNIT * WAYS2 * chunks)
-    start, wait = arrivals(
-        chunks, ((val_hbm, val_ref, 0), (obs_hbm, obs_ref, 0), (pt_hbm, pt_ref, 0)), sems
-    )
-    for c in range(AHEAD):
-        start(c)
     per = pts_refs[0].shape[1] // 16
     for slot, pts_ref in enumerate(pts_refs):
         base = lax.rem(me_ref[0] + len(pts_refs) - slot, len(pts_refs)) * per
@@ -323,9 +289,6 @@
         return pltpu.make_async_copy(res_ref.at[piece, :], res_hbm.at[piece, :], out_sems.at[c])
 
     def chunk(c, total):
-        start(c + AHEAD)
-        wait(c)
-
         def trip(i, total):
             first = (c * trips + i) * WAYS2
             for w in range(WAYS2):
@@ -349,16 +312,31 @@
 
 SMEM = pl.BlockSpec(memory_space=pltpu.SMEM)
 VMEM = pl.BlockSpec(memory_space=pltpu.VMEM)
-HBM = pl.BlockSpec(memory_space=pl.ANY)
+HBM = pl.BlockSpec(memory_space=pltpu.HBM)
+ANY = pl.BlockSpec(memory_space=pl.ANY)
+
+
+def offer_kernel(increment_ref, cameras_ref, out_ref):
+    mine = jnp.concatenate([increment_ref[...], cameras_ref[...]], axis=0)
+    out_ref[...] = jnp.broadcast_to(mine[None], out_ref.shape)
+
+
+def run_offer(increment, cameras, receivers):
+    rows = increment.shape[0] + cameras.shape[0]
+    return pl.pallas_call(
+        offer_kernel,
+        out_shape=jax.ShapeDtypeStruct((receivers, rows, increment.shape[1]), jnp.float32),
+        name="offer_cameras",
+    )(increment, cameras)
 
 
 def run_reduce(me, n_cam, tile_block, tile_points, table, cam_jac, point_jac, ids_cam, ids_pt, points):
     chunks = math.gcd(tile_block.shape[0] // (UNIT * WAYS), CHUNKS)
-    streamed = (cam_jac, point_jac, ids_cam, ids_pt)
+    streamed = (cam_jac, point_jac)
     return pl.pallas_call(
         functools.partial(reduce_kernel, n_cam),
         out_shape=(jax.ShapeDtypeStruct((3, points // 128 // n_cam, 128), jnp.float32),) * n_cam,
-        in_specs=[SMEM] * 3 + [VMEM] + [HBM] * 4,
+        in_specs=[SMEM] * 3 + [VMEM] + [HBM] * 2 + [VMEM] * 2,
         out_specs=(VMEM,) * n_cam,
         scratch_shapes=[pltpu.VMEM(a.shape, a.dtype) for a in streamed]
         + [pltpu.SemaphoreType.DMA((chunks, len(streamed)))]
@@ -367,33 +345,27 @@
         + [pltpu.VMEM((2 * UNIT * PITCH, 128), jnp.float32)] * WAYS
         + [pltpu.VMEM((80, 128), jnp.float32)] * WAYS
         + [pltpu.VMEM((96, 128), jnp.float32)] * WAYS,
+        compiler_params=pltpu.CompilerParams(vmem_limit_bytes=58 << 20),
         name="reduce_points",
-    )(me, tile_block, tile_points, table, *streamed)
+    )(me, tile_block, tile_points, table, *streamed, ids_cam, ids_pt)
 
 
 def run_look(after, tile_block, table, ids_cam):
-    chunks = math.gcd(tile_block.shape[0] // (UNIT * WAYS3), CHUNKS)
     rows = ids_cam.shape[0] * LOOKED
     return pl.pallas_call(
         look_kernel,
         out_shape=jax.ShapeDtypeStruct((rows, 128), jnp.float32),
-        in_specs=[HBM, SMEM, VMEM, HBM],
-        out_specs=HBM,
-        scratch_shapes=[
-            pltpu.VMEM(ids_cam.shape, ids_cam.dtype),
-            pltpu.VMEM((rows, 128), jnp.float32),
-            pltpu.SemaphoreType.DMA((chunks, 1)),
-            pltpu.SemaphoreType.DMA((chunks,)),
-        ]
-        + [pltpu.VMEM((144, 128), jnp.float32)] * WAYS3,
+        in_specs=[ANY, SMEM, VMEM, VMEM],
+        out_specs=VMEM,
+        scratch_shapes=[pltpu.VMEM((144, 128), jnp.float32)] * WAYS3,
         cost_estimate=pl.CostEstimate(flops=WORK, bytes_accessed=rows * 512, transcendentals=0),
+        compiler_params=pltpu.CompilerParams(vmem_limit_bytes=24 << 20),
         name="look_up_cameras",
     )(after, tile_block, table, ids_cam)
 
 
 def run_project(me, senders, tile_points, trial, values, obs_rows, ids_pt):
     chunks = math.gcd(tile_points.shape[0] // (UNIT * WAYS2), CHUNKS)
-    streamed = (values, obs_rows, ids_pt)
     n_cam = len(trial)
     points = n_cam * trial[0].shape[1]
     return pl.pallas_call(
@@ -402,15 +374,14 @@
             jax.ShapeDtypeStruct(obs_rows.shape, jnp.float32),
             jax.ShapeDtypeStruct((senders, 1, 128), jnp.float32),
         ),
-        in_specs=[SMEM] * 2 + [VMEM] * n_cam + [HBM] * 3,
+        in_specs=[SMEM] * 2 + [VMEM] * (n_cam + 3),
         out_specs=(HBM, VMEM),
-        scratch_shapes=[pltpu.VMEM(a.shape, a.dtype) for a in streamed]
-        + [pltpu.VMEM(obs_rows.shape, jnp.float32)]
-        + [pltpu.SemaphoreType.DMA((chunks, len(streamed))), pltpu.SemaphoreType.DMA((chunks,))]
+        scratch_shapes=[pltpu.VMEM(obs_rows.shape, jnp.float32), pltpu.SemaphoreType.DMA((chunks,))]
         + [pltpu.VMEM((points * 4, 128), jnp.float32)]
         + [pltpu.VMEM((72, 128), jnp.float32)] * WAYS2,
+        compiler_params=pltpu.CompilerParams(vmem_limit_bytes=28 << 20),
         name="project_points",
-    )(me, tile_points, *trial, *streamed)
+    )(me, tile_points, *trial, values, obs_rows, ids_pt)
 
 
 def trial_rows(cameras, increment):
@@ -448,10 +419,7 @@
     accept,
 ):
     both = ("pts", "cam")
-    mine = jnp.concatenate([increment, cameras], axis=0)
-    table = lax.all_to_all(
-        jnp.broadcast_to(mine[None], (n_pts * n_cam,) + mine.shape), both, 0, 0
-    )
+    table = lax.all_to_all(run_offer(increment, cameras, n_pts * n_cam), both, 0, 0)
     blocks = table.shape[0] * table.shape[2] // CB
     table = table.reshape(table.shape[0], 18, -1, CB).transpose(0, 2, 1, 3).reshape(blocks, 18, CB)
     looked_table = trial_rows(table[:, 9:18], table[:, 0:9])

time: 104 us -> 99.6 us (0.958)
  Pallas kernels: 34.1 us -> 29.9 us
  waiting for transfers between devices: 24.5 us -> 27.9 us
  other arithmetic: 7.94 us -> 5.32 us
    pallas_call x1, Pallas kernels: 9.45 us -> 5.7 us  [run_project(): pl.pallas_call(functools.partial(project_kernel, n_cam), out_shape=(jax.S...]
    pallas_call x1, Pallas kernels: 8.03 us -> 5.55 us  [run_look(): pl.pallas_call(look_kernel, out_shape=jax.ShapeDtypeStruct((rows, 128), j...]
    ppermute x3, waiting for transfers between devices: 6.42 us -> 8.62 us  [on_device(): lax.ppermute(parts[s], 'cam', [(k, (k + s) % n_cam) for k in range(n_cam)])]
    pallas_call x0 -> x1, Pallas kernels: none -> 1.57 us  [run_offer(): pl.pallas_call(offer_kernel, out_shape=jax.ShapeDtypeStruct((receivers, r...]
    all_to_all x1, waiting for transfers between devices: 3.53 us -> 4.65 us  [on_device(): spread_sums = lax.all_to_all(partial, both, 0, 0)]
    another operation x1, other arithmetic: 1.17 us -> 0.05 us  [on_device(): jnp.stack(trial)]
    unnamed x16 -> x18, local copies, waits for them, and re-layouts: 2.56 us -> 2.75 us
  transfers between devices with their start and end apart: 8 -> 8, of which waited for: 5 -> 5; matrix products, arithmetic and copies ran while one was open for 12% -> 11% of each run, Pallas kernels for 8% -> 6%
where the time goes in v4:
time: 99.6 us; the launch traced here: 99.1 us
  Pallas kernels  29.9 us (30%)
  waiting for transfers between devices  27.9 us (28%)
  starting transfers between devices  24.9 us (25%)
  local copies, waits for them, and re-layouts  7.69 us (8%)
  other arithmetic  5.32 us (5%)
  between operations  3.32 us (3%)
    pallas_call x1, Pallas kernels, run_reduce(): pl.pallas_call(functools.partial(reduce_kernel, n_cam), out_shape=(jax.Sh...  17.1 us
    ppermute x3, waiting for transfers between devices, spread(): lax.ppermute(value, axis, [(k, (k + s) % size) for k in range(size)])  10.2 us
    ppermute x3, waiting for transfers between devices, on_device(): lax.ppermute(parts[s], 'cam', [(k, (k + s) % n_cam) for k in range(n_cam)])  8.62 us
    all_to_all x1, starting transfers between devices, on_device(): spread_sums = lax.all_to_all(partial, both, 0, 0)  8.17 us
    all_to_all x1, starting transfers between devices, on_device(): lax.all_to_all(run_offer(increment, cameras, n_pts * n_cam), both, 0, 0)  7.33 us
    ppermute x3, starting transfers between devices, spread(): lax.ppermute(value, axis, [(k, (k + s) % size) for k in range(size)])  5.74 us
    pallas_call x1, Pallas kernels, run_project(): pl.pallas_call(functools.partial(project_kernel, n_cam), out_shape=(jax.S...  5.7 us
    pallas_call x1, Pallas kernels, run_look(): pl.pallas_call(look_kernel, out_shape=jax.ShapeDtypeStruct((rows, 128), j...  5.55 us
  transfers between devices with their start and end apart: 8, of which 5 were waited for; matrix products, arithmetic and copies ran while one was open for 11% of the time, Pallas kernels for 6%

profile of v4, /device:TPU:0, one launch (start us, length us, event | category | flops | bytes accessed | tf_op | source)
XLA Modules:
  0.0 99.1 jit_solution(7729872600704754550)
XLA Ops:
  0.6 0.0 copy-start
  0.6 1.6 %offer_cameras.1 = f32[32,18,128]{2,1,0:T(8,128)} custom-call(f32[9,128]{1,0:T(8,128)} %increment_ref.1, f32[9,128]{1,0:T(8,128)} %cameras_ref.1), custom_call_target="tpu_custom_call" | custom-call | tf_op jit(solution)/shard_map/offer_cameras/pallas_call | solution.py:326
  2.2 7.3 %all-to-all-start = ((f32[32,18,128]{2,1,0:T(8,128)}), f32[32,18,128]{2,1,0:T(8,128)S(1)}, u32[]{:S(2)}, u32[]{:S(2)}) async-start(f32[32,18,128]{2,1,0:T(8,128)} %offer_cameras.1), calls=%async_computation | async-start | bytes 786432 | tf_op jit(solution)/shard_map/all_to_all | solution.py:422
  10.3 4.3 %constant_dynamic-slice_fusion = (f32[1,16384]{1,0:T(1,128)S(1)}, f32[1,16384]{1,0:T(1,128)S(1)}, f32[1,16384]{1,0:T(1,128)S(1)}, f32[1,16384]{1,0:T(1,128)S(1)}...) fusion(f32[9,65536]{1,0:T(8,128)} %param.17, ...), kind=kLoop, calls=%fused_computation.54 | loop fusion | bytes 1179684 | tf_op jit(solution)/shard_map/slice | solution.py:453
  14.6 0.0 copy-done
  14.6 0.1 dynamic-slice_bitcast_fusion
  14.6 1.0 %dynamic-slice_bitcast_fusion.1 = f32[1,3,128,128]{3,1,2,0:T(4,128)S(1)} fusion(f32[3,65536]{1,0:T(4,128)} %param.15, s32[]{:T(128)S(6)} %select_n.108), kind=kLoop, calls=%fused_computation.9 | loop fusion | bytes 393220
  15.6 1.3 %multiply_add_fusion.4 = f32[9,128]{1,0:T(8,128)} fusion(f32[9,128]{1,0:T(8,128)} %cameras_ref.1, f32[9,128]{1,0:T(8,128)} %increment_ref.1, f32[]{:T(128)S(6)} %convert_element_type.10), kind=kLoop, calls=%fused_computation.43 | loop fusion | flops 2304 | bytes 13828 | tf_op jit(solution)/shard_map/add | solution.py:473
  17.0 4.4 %all-to-all-done.tab_ref = f32[32,18,128]{2,1,0:T(8,128)S(1)} async-done(((f32[32,18,128]{2,1,0:T(8,128)}), f32[32,18,128]{2,1,0:T(8,128)S(1)}, u32[]{:S(2)}, u32[]{:S(2)}) %all-to-all-start) | async-done | bytes 294944 | tf_op jit(solution)/shard_map/all_to_all | solution.py:422
  21.4 0.0 copy-start.7
  21.4 0.7 copy-done.7
  22.1 0.0 copy-start.2
  22.1 0.0 copy-start.5
  22.1 17.1 %reduce_points.1 = (f32[3,128,128]{2,1,0:T(8,128)}, f32[3,128,128]{2,1,0:T(8,128)}, f32[3,128,128]{2,1,0:T(8,128)}, f32[3,128,128]{2,1,0:T(8,128)}) custom-call(s32[1]{0:T(128)} %bitcast.me_ref, s32[1024]{0:T(1024)} %tb_ref.3, s32[1024]{0:T(1024)} %tp_ref.3, f32[32,18,128]{2,1,0:T(8,128)} %copy-done.7, bf16[18,262144]{1,0:T(8,128)(2,1)} %cj_hbm.1, ...), custom_call_target="tpu_custom_call" | custom-call | tf_op jit(solution)/shard_map/reduce_points/pallas_call | solution.py:336
  39.3 2.6 %collective-permute-start.2 = (f32[3,128,128]{2,1,0:T(8,128)}, f32[3,128,128]{2,1,0:T(8,128)S(1)}, u32[]{:S(2)}, u32[]{:S(2)}) collective-permute-start(f32[3,128,128]{2,1,0:T(8,128)} %get-tuple-element.13), channel_id=1, source_target_pairs={{0,3},{1,0},{2,1},{3,2},{4,7},{5,4},{6,5},{7,6},{8,11},{9,8},{10,9... | collective-permute-start | bytes 589832 | tf_op jit(solution)/shard_map/ppermute | solution.py:439
  41.9 1.1 %collective-permute-start.1 = (f32[3,128,128]{2,1,0:T(8,128)}, f32[3,128,128]{2,1,0:T(8,128)S(1)}, u32[]{:S(2)}, u32[]{:S(2)}) collective-permute-start(f32[3,128,128]{2,1,0:T(8,128)} %get-tuple-element.12), channel_id=1, source_target_pairs={{0,2},{1,3},{2,0},{3,1},{4,6},{5,7},{6,4},{7,5},{8,10},{9,11},{10,... | collective-permute-start | bytes 589832 | tf_op jit(solution)/shard_map/ppermute | solution.py:439
  43.0 0.0 collective-permute-start
  43.0 1.1 %slice_add_fusion = f32[32,9,128]{2,1,0:T(8,128)S(1)} fusion(f32[32,18,128]{2,1,0:T(8,128)} %copy-done.7), kind=kLoop, calls=%fused_computation.7 | loop fusion | flops 36864 | bytes 442368 | tf_op jit(solution)/shard_map/add | solution.py:388
  44.1 0.1 fusion.12
  44.2 0.1 select_maximum_fusion.tab_ref
  44.3 0.0 copy-done.2
  44.3 0.0 copy-done.5
  44.3 0.0 copy-start.4
  44.4 0.9 copy-done.4
  45.3 5.5 %look_up_cameras.1.refs_4_ = f32[20480,128]{1,0:T(8,128)S(1)} custom-call(f32[3,128,128]{2,1,0:T(8,128)S(1)} %copy-done.4, s32[1024]{0:T(1024)S(1)} %copy-done.5, f32[32,16,128]{2,1,0:T(8,128)S(1)} %select_maximum_fusion.tab_ref, s32[2048,128]{1,0:T(8,128)S(1)} %bitcast.52), custom_call_target="tpu_custom_call" | custom-call | flops 16777216 | bytes 10485760 | tf_op jit(solution)/shard_map/look_up_cameras/pallas_call | solution.py:355
  50.8 0.0 copy-start.3
  50.8 0.0 collective-permute-done.2
  50.9 8.6 %collective-permute-done.1 = f32[3,128,128]{2,1,0:T(8,128)S(1)} collective-permute-done((f32[3,128,128]{2,1,0:T(8,128)}, f32[3,128,128]{2,1,0:T(8,128)S(1)}, u32[]{:S(2)}, u32[]{:S(2)}) %collective-permute-start.1) | collective-permute-done | bytes 196640 | tf_op jit(solution)/shard_map/ppermute | solution.py:439
  59.5 0.0 collective-permute-done
  59.5 0.1 bitcast_subtract_fusion
  59.6 1.0 %collective-permute-start.3 = (f32[3,128,128]{2,1,0:T(8,128)S(1)}, f32[3,128,128]{2,1,0:T(8,128)S(1)}, u32[]{:S(2)}, u32[]{:S(2)}) collective-permute-start(f32[3,128,128]{2,1,0:T(8,128)S(1)} %bitcast_add_fusion.1.refs_0_), channel_id=1, source_target_pairs={{0,1},{1,2},{2,3},{3,0},{4,5},{5,6},{6,7},{7,4},{8,9},{9,10},{10,1... | collective-permute-start | bytes 589832 | tf_op jit(solution)/shard_map/ppermute | solution.py:400
  60.6 1.9 %collective-permute-start.4 = (f32[3,128,128]{2,1,0:T(8,128)S(1)}, f32[3,128,128]{2,1,0:T(8,128)S(1)}, u32[]{:S(2)}, u32[]{:S(2)}) collective-permute-start(f32[3,128,128]{2,1,0:T(8,128)S(1)} %bitcast_add_fusion.1.refs_0_), channel_id=1, source_target_pairs={{0,2},{1,3},{2,0},{3,1},{4,6},{5,7},{6,4},{7,5},{8,10},{9,11},{10,... | collective-permute-start | bytes 589832 | tf_op jit(solution)/shard_map/ppermute | solution.py:400
  62.5 2.8 %collective-permute-start.5 = (f32[3,128,128]{2,1,0:T(8,128)S(1)}, f32[3,128,128]{2,1,0:T(8,128)S(1)}, u32[]{:S(2)}, u32[]{:S(2)}) collective-permute-start(f32[3,128,128]{2,1,0:T(8,128)S(1)} %bitcast_add_fusion.1.refs_0_), channel_id=1, source_target_pairs={{0,3},{1,0},{2,1},{3,2},{4,7},{5,4},{6,5},{7,6},{8,11},{9,8},{10,9... | collective-permute-start | bytes 589832 | tf_op jit(solution)/shard_map/ppermute | solution.py:400
  65.4 3.3 %collective-permute-done.3.refs_1_ = f32[3,128,128]{2,1,0:T(8,128)S(1)} collective-permute-done((f32[3,128,128]{2,1,0:T(8,128)S(1)}, f32[3,128,128]{2,1,0:T(8,128)S(1)}, u32[]{:S(2)}, u32[]{:S(2)}) %collective-permute-start.3) | collective-permute-done | bytes 196640 | tf_op jit(solution)/shard_map/ppermute | solution.py:400
  68.7 6.9 %collective-permute-done.4.refs_2_ = f32[3,128,128]{2,1,0:T(8,128)S(1)} collective-permute-done((f32[3,128,128]{2,1,0:T(8,128)S(1)}, f32[3,128,128]{2,1,0:T(8,128)S(1)}, u32[]{:S(2)}, u32[]{:S(2)}) %collective-permute-start.4) | collective-permute-done | bytes 196640 | tf_op jit(solution)/shard_map/ppermute | solution.py:400
  75.6 0.0 collective-permute-done.5.refs_3_
  75.6 0.0 copy-done.6
  75.6 0.0 copy-done.1
  75.6 0.0 copy-done.3
  75.6 5.7 %project_points.1 = (f32[4096,128]{1,0:T(8,128)}, f32[32,1,128]{2,1,0:T(1,128)}) custom-call(s32[1]{0:T(128)} %bitcast.me_ref, s32[1024]{0:T(1024)S(1)} %copy-done.6, f32[3,128,128]{2,1,0:T(8,128)S(1)} %bitcast_add_fusion.1.refs_0_, f32[3,128,128]{2,1,0:T(8,128)S(1)} %collective-permute-done.3.refs_1_, f32[3,128,128]{2,1,0:T(8,128)S(1)} %collective-permute-done.4.refs_2_, ...), custom_call_target="tpu_custom_call" | custom-call | tf_op jit(solution)/shard_map/project_points/pallas_call | solution.py:371
  81.3 8.2 %all-to-all-start.1 = ((f32[32,1,128]{2,1,0:T(1,128)}), f32[32,1,128]{2,1,0:T(1,128)S(1)}, u32[]{:S(2)}, u32[]{:S(2)}) async-start(f32[32,1,128]{2,1,0:T(1,128)} %get-tuple-element.15), calls=%async_computation.1 | async-start | bytes 32768 | tf_op jit(solution)/shard_map/all_to_all | solution.py:467
  89.5 0.1 pad_maximum_fusion
  89.6 0.6 gather_fusion
  90.2 0.1 select_bitcast_fusion
  90.3 0.1 copy.21
  90.4 1.7 %bitcast_select_fusion = f32[3,65536]{1,0:T(4,128)} fusion(f32[3,65536]{1,0:T(4,128)} %param.15, f32[1,3,512,128]{3,2,1,0:T(8,128)S(1)} %bitcast.57, pred[]{:T(512)S(6)} %gt.3), kind=kLoop, calls=%fused_computation.1 | loop fusion | flops 196608 | bytes 2359297 | tf_op jit(solution)/shard_map/jit(_where)/select_n | solution.py:472
  92.1 4.7 %all-to-all-done.1 = f32[32,1,128]{2,1,0:T(1,128)S(1)} async-done(((f32[32,1,128]{2,1,0:T(1,128)}), f32[32,1,128]{2,1,0:T(1,128)S(1)}, u32[]{:S(2)}, u32[]{:S(2)}) %all-to-all-start.1) | async-done | bytes 16416 | tf_op jit(solution)/shard_map/all_to_all | solution.py:467
  96.7 0.6 reduce_sum.19
  (11 shorter events, 0.2 us)
Async XLA Ops:
  0.6 13.9 %copy-start = (f32[3,65536]{1,0:T(4,128)S(1)}, f32[3,65536]{1,0:T(4,128)}, u32[]{:S(2)}) copy-start(f32[3,65536]{1,0:T(4,128)} %param.16) | copy-start | bytes 2359300
  2.2 19.2 %all-to-all-start = ((f32[32,18,128]{2,1,0:T(8,128)}), f32[32,18,128]{2,1,0:T(8,128)S(1)}, u32[]{:S(2)}, u32[]{:S(2)}) async-start(f32[32,18,128]{2,1,0:T(8,128)} %offer_cameras.1), calls=%async_computation | async-start | bytes 786432 | tf_op jit(solution)/shard_map/all_to_all | solution.py:422
  21.4 0.7 copy-start.7
  22.1 22.2 %copy-start.2 = (s32[262144]{0:T(1024)S(1)}, s32[262144]{0:T(1024)}, u32[]{:S(2)}) copy-start(s32[262144]{0:T(1024)} %param.23) | copy-start | bytes 3145732
  22.1 22.2 %copy-start.5 = (s32[1024]{0:T(1024)S(1)}, s32[1024]{0:T(1024)}, u32[]{:S(2)}) copy-start(s32[1024]{0:T(1024)} %tb_ref.3) | copy-start | bytes 12292
  39.3 11.6 %collective-permute-start.2 = (f32[3,128,128]{2,1,0:T(8,128)}, f32[3,128,128]{2,1,0:T(8,128)S(1)}, u32[]{:S(2)}, u32[]{:S(2)}) collective-permute-start(f32[3,128,128]{2,1,0:T(8,128)} %get-tuple-element.13), channel_id=1, source_target_pairs={{0,3},{1,0},{2,1},{3,2},{4,7},{5,4},{6,5},{7,6},{8,11},{9,8},{10,9... | collective-permute-start | bytes 589832 | tf_op jit(solution)/shard_map/ppermute | solution.py:439
  41.9 17.6 %collective-permute-start.1 = (f32[3,128,128]{2,1,0:T(8,128)}, f32[3,128,128]{2,1,0:T(8,128)S(1)}, u32[]{:S(2)}, u32[]{:S(2)}) collective-permute-start(f32[3,128,128]{2,1,0:T(8,128)} %get-tuple-element.12), channel_id=1, source_target_pairs={{0,2},{1,3},{2,0},{3,1},{4,6},{5,7},{6,4},{7,5},{8,10},{9,11},{10,... | collective-permute-start | bytes 589832 | tf_op jit(solution)/shard_map/ppermute | solution.py:439
  43.0 16.5 %collective-permute-start = (f32[3,128,128]{2,1,0:T(8,128)}, f32[3,128,128]{2,1,0:T(8,128)S(1)}, u32[]{:S(2)}, u32[]{:S(2)}) collective-permute-start(f32[3,128,128]{2,1,0:T(8,128)} %get-tuple-element.11), channel_id=1, source_target_pairs={{0,1},{1,2},{2,3},{3,0},{4,5},{5,6},{6,7},{7,4},{8,9},{9,10},{10,1... | collective-permute-start | bytes 589832 | tf_op jit(solution)/shard_map/ppermute | solution.py:439
  44.3 0.9 copy-start.4
  45.3 30.3 %copy-start.6 = (s32[1024]{0:T(1024)S(1)}, s32[1024]{0:T(1024)}, u32[]{:S(2)}) copy-start(s32[1024]{0:T(1024)} %tp_ref.3) | copy-start | bytes 12292
  50.8 24.8 %copy-start.1 = (s32[262144]{0:T(1024)S(1)}, s32[262144]{0:T(1024)}, u32[]{:S(2)}) copy-start(s32[262144]{0:T(1024)} %param.24) | copy-start | bytes 3145732
  50.8 24.8 %copy-start.3 = (f32[2,262144]{1,0:T(2,128)S(1)}, f32[2,262144]{1,0:T(2,128)}, u32[]{:S(2)}) copy-start(f32[2,262144]{1,0:T(2,128)} %param.20) | copy-start | bytes 6291460
  59.6 9.1 %collective-permute-start.3 = (f32[3,128,128]{2,1,0:T(8,128)S(1)}, f32[3,128,128]{2,1,0:T(8,128)S(1)}, u32[]{:S(2)}, u32[]{:S(2)}) collective-permute-start(f32[3,128,128]{2,1,0:T(8,128)S(1)} %bitcast_add_fusion.1.refs_0_), channel_id=1, source_target_pairs={{0,1},{1,2},{2,3},{3,0},{4,5},{5,6},{6,7},{7,4},{8,9},{9,10},{10,1... | collective-permute-start | bytes 589832 | tf_op jit(solution)/shard_map/ppermute | solution.py:400
  60.6 15.0 %collective-permute-start.4 = (f32[3,128,128]{2,1,0:T(8,128)S(1)}, f32[3,128,128]{2,1,0:T(8,128)S(1)}, u32[]{:S(2)}, u32[]{:S(2)}) collective-permute-start(f32[3,128,128]{2,1,0:T(8,128)S(1)} %bitcast_add_fusion.1.refs_0_), channel_id=1, source_target_pairs={{0,2},{1,3},{2,0},{3,1},{4,6},{5,7},{6,4},{7,5},{8,10},{9,11},{10,... | collective-permute-start | bytes 589832 | tf_op jit(solution)/shard_map/ppermute | solution.py:400
  62.5 13.1 %collective-permute-start.5 = (f32[3,128,128]{2,1,0:T(8,128)S(1)}, f32[3,128,128]{2,1,0:T(8,128)S(1)}, u32[]{:S(2)}, u32[]{:S(2)}) collective-permute-start(f32[3,128,128]{2,1,0:T(8,128)S(1)} %bitcast_add_fusion.1.refs_0_), channel_id=1, source_target_pairs={{0,3},{1,0},{2,1},{3,2},{4,7},{5,4},{6,5},{7,6},{8,11},{9,8},{10,9... | collective-permute-start | bytes 589832 | tf_op jit(solution)/shard_map/ppermute | solution.py:400
  81.3 15.4 %all-to-all-start.1 = ((f32[32,1,128]{2,1,0:T(1,128)}), f32[32,1,128]{2,1,0:T(1,128)S(1)}, u32[]{:S(2)}, u32[]{:S(2)}) async-start(f32[32,1,128]{2,1,0:T(1,128)} %get-tuple-element.15), calls=%async_computation.1 | async-start | bytes 32768 | tf_op jit(solution)/shard_map/all_to_all | solution.py:467
